TPU v7x, 16 devices: a whole 2x2x2 slice. The times are simulated.
16 devices in a mesh: dp: 16 (over z, y, x, core).
Axes of the slice: x: 2, y: 2, z: 2, core: 2. Of those that a mesh axis runs over, the one named last changes fastest.
Arguments:
- grad_embed: bfloat16 [16, 8192, 1152], P('dp')
- grad_q: bfloat16 [16, 6, 1152, 32], P('dp')
- grad_k: bfloat16 [16, 6, 1152, 8], P('dp')
- grad_v: bfloat16 [16, 6, 1152, 8], P('dp')
- grad_out: bfloat16 [16, 6, 32, 1152], P('dp')
- grad_gate: bfloat16 [16, 6, 1152, 216], P('dp')
- grad_up: bfloat16 [16, 6, 1152, 216], P('dp')
- grad_down: bfloat16 [16, 6, 216, 1152], P('dp')
- grad_norms: bfloat16 [16, 6, 4, 1152], P('dp')
- grad_qk_norms: bfloat16 [16, 6, 2, 256], P('dp')
- first_moment: float32 [14499840], P('dp')
- second_moment: float32 [14499840], P('dp')
- master_param: float32 [14499840], P('dp')
- hyper_params: float32 [5], replicated
Outputs:
- output 1: bfloat16 [8192, 1152], replicated
- output 2: bfloat16 [6, 1152, 32], replicated
- output 3: bfloat16 [6, 1152, 8], replicated
- output 4: bfloat16 [6, 1152, 8], replicated
- output 5: bfloat16 [6, 32, 1152], replicated
- output 6: bfloat16 [6, 1152, 216], replicated
- output 7: bfloat16 [6, 1152, 216], replicated
- output 8: bfloat16 [6, 216, 1152], replicated
- output 9: bfloat16 [6, 4, 1152], replicated
- output 10: bfloat16 [6, 2, 256], replicated
- output 11: float32 [14499840], P('dp')
- output 12: float32 [14499840], P('dp')
- output 13: float32 [14499840], P('dp')
All inputs are finite; a program needn't handle non-finite values.
Results may differ from a plain program's by a relative error of at most 0.001.
Values are sent between devices in bfloat16 or wider.
A program may use at most 1 GiB of HBM per device.

v0:
```python
import math
import jax
import jax.numpy as jnp
from jax import lax
from jax.sharding import PartitionSpec as P

ADAM_STEP = 7
ADAM_EPS = 1e-8
CLIP_EPS = 1e-6
GRAD_COUNT = 10
NORM_COUNT = 2


def adam_step(grad_part, first_part, second_part, master_part, hyper_params, clip_scale, keep_decay):
    learn_rate = hyper_params[0]
    beta_one = hyper_params[1]
    beta_two = hyper_params[2]
    weight_decay = hyper_params[3]
    clipped = grad_part * clip_scale
    moment_one = beta_one * first_part + (1.0 - beta_one) * clipped
    moment_two = beta_two * second_part + (1.0 - beta_two) * (clipped * clipped)
    m_hat = moment_one / (1.0 - beta_one ** ADAM_STEP)
    v_hat = moment_two / (1.0 - beta_two ** ADAM_STEP)
    direction = m_hat / (jnp.sqrt(v_hat) + ADAM_EPS) + jnp.where(keep_decay, weight_decay * master_part, 0.0)
    new_master = master_part - learn_rate * direction
    return moment_one, moment_two, new_master


def split_params(joined, shapes):
    pieces = []
    start_pos = 0
    for tensor_dims in shapes:
        tensor_size = math.prod(tensor_dims)
        pieces.append(joined[start_pos:start_pos + tensor_size].reshape(tensor_dims))
        start_pos = start_pos + tensor_size
    return pieces


def solution(mesh):
    group_size = mesh.shape["dp"]

    def local_update(*arrays):
        grads = arrays[:GRAD_COUNT]
        first_part, second_part, master_part, hyper_params = arrays[GRAD_COUNT:]
        shapes = [grad_arr.shape[1:] for grad_arr in grads]
        sizes = [math.prod(tensor_dims) for tensor_dims in shapes]
        total_len = sum(sizes)
        shard_len = total_len // group_size
        decay_len = total_len - sum(sizes[GRAD_COUNT - NORM_COUNT:])
        local_vec = jnp.concatenate([grad_arr.reshape(-1) for grad_arr in grads]).reshape(group_size, shard_len)
        received = lax.all_to_all(local_vec, "dp", 0, 0, tiled=True)
        grad_part = jnp.sum(received, axis=0, dtype=jnp.float32) / group_size
        square_sum = lax.psum(jnp.sum(grad_part * grad_part), "dp")
        clip_scale = jnp.minimum(1.0, hyper_params[4] / (jnp.sqrt(square_sum) + CLIP_EPS))
        offset = lax.axis_index("dp") * shard_len
        keep_decay = offset + lax.broadcasted_iota(jnp.int32, (shard_len,), 0) < decay_len
        moment_one, moment_two, new_master = adam_step(grad_part, first_part, second_part, master_part, hyper_params, clip_scale, keep_decay)
        full_vec = lax.all_gather(new_master.astype(jnp.bfloat16), "dp", tiled=True)
        return tuple(split_params(full_vec, shapes)) + (moment_one, moment_two, new_master)

    in_specs = tuple([P("dp")] * GRAD_COUNT + [P("dp"), P("dp"), P("dp"), P()])
    out_specs = tuple([P()] * GRAD_COUNT + [P("dp"), P("dp"), P("dp")])
    return jax.shard_map(local_update, mesh=mesh, in_specs=in_specs, out_specs=out_specs, check_vma=False)
```

profile of v0, /device:TPU:0, one launch (start us, length us, event | category | flops | bytes accessed | tf_op | source)
XLA Modules:
  0.0 1167.0 jit_solution(16901606984671245150)
XLA Ops:
  7.2 34.2 %reshape.97 = bf16[9437184]{0:T(1024)(128)(2,1)} reshape(bf16[1,8192,1152]{2,1,0:T(8,128)(2,1)} %param.14) | data formatting | bytes 37748736 | tf_op jit(solution)/shard_map/reshape | solution.py:50
  41.3 16.5 %constant_dynamic-update-slice_fusion.9 = bf16[14499840]{0:T(1024)(128)(2,1)} fusion(bf16[9437184]{0:T(1024)(128)(2,1)} %reshape.97), kind=kLoop, calls=%fused_computation.15 | loop fusion | bytes 37748736
  61.6 2.5 reshape.99
  65.1 2.5 reshape.100
  68.8 4.4 copy.40
  73.3 11.8 %reshape.102 = bf16[1492992]{0:T(1024)(128)(2,1)} reshape(bf16[1,6,1152,216]{3,2,1,0:T(8,128)(2,1)S(1)} %copy.40) | data formatting | bytes 5971968 | tf_op jit(solution)/shard_map/reshape | solution.py:50
  85.0 4.5 copy.41
  89.5 11.8 %reshape.103 = bf16[1492992]{0:T(1024)(128)(2,1)} reshape(bf16[1,6,1152,216]{3,2,1,0:T(8,128)(2,1)S(1)} %copy.41) | data formatting | bytes 5971968 | tf_op jit(solution)/shard_map/reshape | solution.py:50
  101.3 5.3 reshape.104
  110.6 1.8 constant_dynamic-update-slice_fusion.6
  113.2 3.3 constant_dynamic-update-slice_fusion.4
  116.5 2.1 constant_dynamic-update-slice_fusion.3
  121.5 31.6 %all_to_all.8 = bf16[16,1,906240]{2,1,0:T(2,128)(2,1)} reshape(bf16[14499840]{0:T(1024)(128)(2,1)} %constant_dynamic-update-slice_fusion) | data formatting | bytes 57999360 | tf_op jit(solution)/shard_map/all_to_all | solution.py:51
  153.7 173.6 %reduce.1 = bf16[16,906240]{1,0:T(8,128)(2,1)} reduce(bf16[16,1,906240]{2,1,0:T(2,128)(2,1)} %all_to_all.8, bf16[]{:T(256)} %broadcast.2), dimensions={1}, to_apply=%all_to_all.8.reduce_sub_computation | reduce | bytes 57999360 | tf_op jit(solution)/shard_map/all_to_all | solution.py:51
  327.2 99.8 %reshape.116 = bf16[16,2,453120]{2,1,0:T(2,128)(2,1)} reshape(bf16[16,906240]{1,0:T(8,128)(2,1)} %reduce.1) | data formatting | bytes 57999360
  427.0 5.3 all-to-all-start
  438.2 344.5 %all-to-all-done = bf16[16,2,453120]{2,1,0:T(2,128)(2,1)} async-done(((bf16[16,2,453120]{2,1,0:T(2,128)(2,1)}), bf16[16,2,453120]{2,1,0:T(2,128)(2,1)}, u32[]{:S(2)}, u32[]{:S(2)}) %all-to-all-start) | async-done | bytes 28999712 | tf_op jit(solution)/shard_map/all_to_all | solution.py:51
  782.7 36.2 %reshape.117 = bf16[16,1,906240]{2,1,0:T(2,128)(2,1)} reshape(bf16[16,2,453120]{2,1,0:T(2,128)(2,1)} %all-to-all-done) | data formatting | bytes 57999360
  818.9 63.4 %convert_reduce_fusion = f32[906240]{0:T(1024)S(1)} fusion(bf16[16,1,906240]{2,1,0:T(2,128)(2,1)} %reshape.117), kind=kLoop, calls=%fused_computation | loop fusion | flops 28093440 | bytes 32624640 | tf_op jit(solution)/shard_map/reduce_sum | solution.py:52
  885.6 34.6 %psum.7 = f32[]{:T(128)} all-reduce(f32[]{:T(128)} %multiply_reduce_fusion), channel_id=1, replica_groups=mesh['dp'=16] {'dp'}, use_global_device_ids=true, to_apply=%region_2.0 | all-reduce | flops 1 | bytes 8 | tf_op jit(solution)/shard_map/psum | solution.py:53
  921.6 12.0 %fusion = (bf16[906240]{0:T(1024)(128)(2,1)}, f32[906240]{0:T(1024)}, f32[906240]{0:T(1024)}, f32[906240]{0:T(1024)}) fusion(f32[906240]{0:T(1024)} %param.26, f32[]{:T(128)} %bitcast.4, s32[]{:T(128)S(6)} %mul.99, f32[]{:T(128)S(6)} %sub.18, f32[]{:T(128)S(6)} %sub.16, f32[]{:T(128)} %bitcast, f32[906240]{0:T(1024)} %copy-done, f32[]{:T(128)S(6)} %mul.82, ...), kind=kLoop, calls=%fused_computation.16 | loop fusion | flops 18124800 | bytes 27187240 | tf_op jit(solution)/shard_map/convert_element_type | solution.py:58
  933.6 117.8 %all-gather.2.cloned.1.call-done = bf16[14499840]{0:T(1024)(128)(2,1)} async-done(((bf16[906240]{0:T(1024)(128)(2,1)}), bf16[14499840]{0:T(1024)(128)(2,1)}) %all-gather.2.cloned.1.call-update) | async-done | bytes 28999696 | tf_op jit(solution)/shard_map/all_gather | solution.py:58
  1051.4 16.4 %slice.71 = bf16[9437184]{0:T(1024)(128)(2,1)} slice(bf16[14499840]{0:T(1024)(128)(2,1)} %all-gather.2.cloned.1.call-done), slice={[0:9437184]} | slice | bytes 37748736 | tf_op jit(solution)/shard_map/slice | solution.py:34
  1067.9 35.2 %reshape.107 = bf16[8192,1152]{1,0:T(8,128)(2,1)} reshape(bf16[9437184]{0:T(1024)(128)(2,1)} %slice.71) | data formatting | bytes 37748736 | tf_op jit(solution)/shard_map/reshape | solution.py:34
  1107.4 1.9 reshape.109
  1110.7 1.9 reshape.110
  1115.2 6.3 fusion.1
  1121.5 11.6 reshape.112
  1133.1 3.6 copy.46
  1136.7 11.6 reshape.113
  1148.3 3.6 copy.47
  1151.8 6.6 reshape.114
  (53 shorter events, 27.6 us)
Async XLA Ops:
  41.3 16.5 %copy-start.5 = (bf16[1,6,1152,32]{2,3,1,0:T(8,128)(2,1)S(1)}, bf16[1,6,1152,32]{2,3,1,0:T(8,128)(2,1)}, u32[]{:S(2)}) copy-start(bf16[1,6,1152,32]{2,3,1,0:T(8,128)(2,1)} %param.15) | copy-start | bytes 1327108
  57.9 2.6 copy-start.7
  57.9 6.2 copy-start.8
  60.5 7.1 copy-start.3
  101.3 6.8 copy-start.10
  101.3 8.6 copy-start.4
  101.3 11.1 copy-start.2
  109.9 6.6 copy-start.1
  118.6 1.7 copy-start.6
  427.0 5.4 copy-start.9
  427.0 355.7 %all-to-all-start = ((bf16[16,2,453120]{2,1,0:T(2,128)(2,1)}), bf16[16,2,453120]{2,1,0:T(2,128)(2,1)}, u32[]{:S(2)}, u32[]{:S(2)}) async-start(bf16[16,2,453120]{2,1,0:T(2,128)(2,1)} %reshape.116), calls=%async_computation | async-start | bytes 57999360 | tf_op jit(solution)/shard_map/all_to_all | solution.py:51
  432.4 619.1 %all-gather.2.cloned.1.call-start = ((), (), s32[]{:S(2)}) async-start(), calls=%async_computation.1 | async-start | bytes 30812160 | tf_op jit(solution)/shard_map/all_gather | solution.py:58
  882.3 1.8 copy-start
  1151.8 6.6 slice-start
  1151.8 7.3 slice-start.1
Sparse Core Ops, SparseCore 0:
  933.7 117.6 all-gather.1
where the time goes:
time: 1180 us; the launch traced here: 1170 us
  waiting for transfers between devices  462 us (39%)
  local copies, waits for them, and re-layouts  393 us (33%)
  other arithmetic  251 us (21%)
  blocking collectives  34.6 us (3%)
  between operations  21.2 us (2%)
    all_to_all x1, waiting for transfers between devices, local_update(): received = lax.all_to_all(local_vec, 'dp', 0, 0, tiled=True)  345 us
    unnamed x44, local copies, waits for them, and re-layouts  190 us
    all_to_all x1, other arithmetic, local_update(): received = lax.all_to_all(local_vec, 'dp', 0, 0, tiled=True)  174 us
    all_gather x1, waiting for transfers between devices, local_update(): full_vec = lax.all_gather(new_master.astype(jnp.bfloat16), 'dp', tiled=True)  118 us
    reshape x9, local copies, waits for them, and re-layouts, local_update(): grad_arr.reshape(-1)  72.3 us
    reshape x9, local copies, waits for them, and re-layouts, split_params(): joined[start_pos:start_pos + tensor_size].reshape(tensor_dims)  71.6 us
    reduce_sum x1, other arithmetic, local_update(): grad_part = jnp.sum(received, axis=0, dtype=jnp.float32) / group_size  63.4 us
    psum x1, blocking collectives, local_update(): square_sum = lax.psum(jnp.sum(grad_part * grad_part), 'dp')  34.6 us
  transfers between devices with their start and end apart: 2, of which 2 were waited for; matrix products, arithmetic and copies ran while one was open for 0% of the time, Pallas kernels for 0%

commit v1 on v0

v1 whole, which is shorter than its diff:
```python
import functools
import jax
import jax.numpy as jnp
from jax import lax
from jax.experimental import pallas as pl
from jax.experimental.pallas import tpu as pltpu
from jax.sharding import PartitionSpec as P

ADAM_EPS = 1e-8
CLIP_EPS = 1e-6
GRAD_COUNT = 10
MESH = pl.DeviceIdType.MESH

ROWS, LANES = 8, 128
TILE = (ROWS, LANES)
SHARE = 885
WIN = 918
NC = 6
WC = WIN // 3
T = WC // NC
STEP = 17
SMALL = 16 * 1024 * 1024
EMB = 9216
TAIL = 8847
LAY = 5313
LAYP = LAY + 33
HEAD = 21
PUB = 900
PC = PUB // 3
EXT = HEAD + SHARE
OFF_Q, OFF_K, OFF_V, OFF_O = 369, 585, 639, 693
OFF_G, OFF_U, OFF_D, OFF_N = 909, 2367, 3825, 5283
DIM = (2, 4, 8)
SHIFT = 88


def start_of(s):
    return 9 * ((SHARE * s) // 9) - jnp.where(s == 13, 18, 0) - jnp.where(s == 14, 9, 0)


def axes(colour):
    return [(colour + n) % 3 for n in range(3)]


def bit(d, dim):
    return (d // DIM[dim]) % 2


def flip(d, dim):
    return d + DIM[dim] * (1 - 2 * bit(d, dim))


def copies_wait(ref, sem):
    pltpu.make_async_copy(ref, ref, sem).wait()


def lanes():
    return lax.broadcasted_iota(jnp.int32, TILE, 1)


def gate_segments():
    rows = []
    for kap in range(27):
        pieces, f = [], LANES * kap
        while f < LANES * (kap + 1):
            i, c = f // 216, f % 216
            pieces.append((f - LANES * kap, i, c // LANES))
            f = min(LANES * (kap + 1), 216 * i + (128 if c < 128 else 216))
        rows.append(pieces)
    return rows


def gate_inverse():
    table = {}
    for kap, pieces in enumerate(gate_segments()):
        for n, (lo, i, half) in enumerate(pieces):
            hi = pieces[n + 1][0] if n + 1 < len(pieces) else 128
            table.setdefault((i, half), []).append((lo, hi, kap))
    return table


def merge(pieces, ids):
    out = pieces[0][1]
    for lo, val in pieces[1:]:
        out = jnp.where(ids >= lo, val, out)
    return out


def rows9_to_flat(win, flat, tmp, o, f):
    for ct in range(9):
        flat[pl.ds(f * ROWS + ct, ROWS, 9), :] = win[o + ct]


def gate_to_flat(win, flat, tmp, o, f):
    for half in range(2):
        tmp[half] = win[pl.ds(o + 16 * half, 16)].reshape(LANES, LANES).T
    ids = lanes()
    rolled = {}
    for i in range(16):
        for half in range(2):
            x = tmp[half, pl.ds(i, ROWS, 16), :]
            rolled[i, half] = pltpu.roll(x, (SHIFT * i) % LANES, 1)
    for kap, pieces in enumerate(gate_segments()):
        val = merge([(lo, rolled[i, half]) for lo, i, half in pieces], ids)
        flat[pl.ds(f * ROWS + kap, ROWS, 27), :] = val


def swap_groups(xs, width):
    ids = lanes() // width
    xs, step = list(xs), 1
    while step < len(xs):
        high = (ids // step) % 2 == 1
        for n in range(len(xs)):
            if not n & step:
                lo, hi = xs[n], xs[n + step]
                xs[n] = jnp.where(high, pltpu.roll(hi, width * step, 1), lo)
                xs[n + step] = jnp.where(high, hi, pltpu.roll(lo, LANES - width * step, 1))
        step = 2 * step
    return xs


def q_to_flat(win, flat, tmp, o, f):
    tmp[0] = win[pl.ds(o, 16)].reshape(LANES, LANES).T
    for kb in range(4):
        xs = swap_groups([tmp[0, pl.ds(32 * kb + i, ROWS, 4), :] for i in range(4)], 32)
        for u in range(4):
            flat[pl.ds((f + 4 * u + kb) * ROWS, ROWS), :] = xs[u]


def kv_to_flat(win, flat, tmp, o, f):
    tmp[0] = win[pl.ds(o, 16)].reshape(LANES, LANES).T
    xs = swap_groups([tmp[0, pl.ds(i, ROWS, 16), :] for i in range(16)], 8)
    for u in range(16):
        flat[pl.ds((f + u) * ROWS, ROWS), :] = xs[u]


def copy_to_flat(win, flat, tmp, o, f):
    flat[pl.ds(f * ROWS, ROWS), :] = win[o]


def rows9_to_tiles(stage, flat, tmp, o, f):
    for ct in range(9):
        stage[o + ct] = flat[pl.ds(f * ROWS + ct, ROWS, 9), :].astype(jnp.bfloat16)


def gate_to_tiles(stage, flat, tmp, o, f):
    ids = lanes()
    rows = [flat[pl.ds(f * ROWS + kap, ROWS, 27), :] for kap in range(27)]
    for (i, half), pieces in gate_inverse().items():
        val = rows[pieces[0][2]]
        for lo, hi, kap in pieces[1:]:
            val = jnp.where((ids >= lo) & (ids < hi), rows[kap], val)
        tmp[half, pl.ds(i, ROWS, 16), :] = pltpu.roll(val, (LANES - SHIFT * i) % LANES, 1)
    stage[pl.ds(o, 16)] = tmp[0].T.reshape(16, ROWS, LANES).astype(jnp.bfloat16)
    stage[pl.ds(o + 16, 11)] = tmp[1].T[:88].reshape(11, ROWS, LANES).astype(jnp.bfloat16)


def q_to_tiles(stage, flat, tmp, o, f):
    for kb in range(4):
        xs = swap_groups([flat[pl.ds((f + 4 * u + kb) * ROWS, ROWS), :] for u in range(4)], 32)
        for i in range(4):
            tmp[0, pl.ds(32 * kb + i, ROWS, 4), :] = xs[i]
    stage[pl.ds(o, 16)] = tmp[0].T.reshape(16, ROWS, LANES).astype(jnp.bfloat16)


def kv_to_tiles(stage, flat, tmp, o, f):
    xs = swap_groups([flat[pl.ds((f + u) * ROWS, ROWS), :] for u in range(16)], 8)
    for i in range(16):
        tmp[0, pl.ds(i, ROWS, 16), :] = xs[i]
    stage[pl.ds(o, 16)] = tmp[0].T.reshape(16, ROWS, LANES).astype(jnp.bfloat16)


def copy_to_tiles(stage, flat, tmp, o, f):
    stage[o] = flat[pl.ds(f * ROWS, ROWS), :].astype(jnp.bfloat16)


def walk_units(me, base, wide, rows9, gate, q, kv, one):
    def pick(table):
        return sum(jnp.where(me == d, n, 0) for d, n in table.items())
    ends = (SHARE * (me + 1) + (8 if wide else 0)) // 9 - (SHARE * me) // 9
    first = jnp.where(me < 10, ends, pick({10: 41, 11: 3, 15: 95}))
    n_q = pick({10: 14})
    n_kv = pick({10: 7})
    n_gate = pick({11: 32, 12: 33 if wide else 32, 13: 34 if wide else 33, 14: 11})
    second = pick({10: 22 if wide else 21, 14: 67})
    n_one = pick({15: 30})
    pos = 0
    for count, size, fn, over in ((first, 9, rows9, 0), (n_q, 16, q, pick({10: 8})), (n_kv, 16, kv, pick({10: 4})),
                                  (n_gate, 27, gate, 0), (second, 9, rows9, 0), (n_one, 1, one, 0)):
        def step(u, carry, pos=pos, size=size, fn=fn):
            fn(pos + u * size, base + pos + u * size)
            return carry
        lax.fori_loop(0, count, step, 0)
        pos = pos + count * size - over


def reduce_kernel(emb, q, k, v, out, gate, up, down, norm, mom, var, mas,
                  flat_out, norm_out, head_out,
                  lay, raw, own, acc, recv2, recv3, flat, tmp, part,
                  lay_sem, head_sems, own_sem, raw_send, raw_recv, s2_send, s2_recv, s3_send, s3_recv, n_send, n_recv, o_sem):
    me = lax.axis_index("dp")
    core = me % 2
    nxt = lax.rem(me + 1, 16)

    for src, off, n in ((emb.at[pl.ds(TAIL, OFF_Q)], 0, OFF_Q), (out, OFF_O, 216), (down, OFF_D, 1458), (norm, OFF_N, 30)):
        pltpu.make_async_copy(src, lay.at[pl.ds(off, n)], lay_sem).start()

    def load(i, carry):
        l, rb = i // 9, lax.rem(i, 9)
        for src, off, n in ((q, OFF_Q, 4), (k, OFF_K, 1), (v, OFF_V, 1), (gate, OFF_G, 27), (up, OFF_U, 27)):
            pltpu.make_async_copy(src.at[l, :, rb], lay.at[pl.ds(off + i * n, n)], lay_sem).start()
        return carry

    lax.fori_loop(0, 54, load, 0)
    lay[pl.ds(LAY, LAYP - LAY)] = jnp.zeros((LAYP - LAY, ROWS, LANES), jnp.bfloat16)

    heads = []
    for n, src in enumerate((mom, var, mas)):
        copy = pltpu.make_async_remote_copy(
            src_ref=src.at[pl.ds(SHARE - HEAD, HEAD)], dst_ref=head_out.at[n], send_sem=head_sems.at[0, n], recv_sem=head_sems.at[1, n],
            device_id=(nxt,), device_id_type=MESH)
        copy.start()
        heads.append(copy)

    def send_raw(s, pos, dst, target, recv_sem, turn):
        first = start_of(s) + pos

        def send(src):
            pltpu.make_async_remote_copy(
                src_ref=src, dst_ref=dst, send_sem=raw_send, recv_sem=recv_sem, device_id=(target,), device_id_type=MESH).start()

        @pl.when((s < 10) & (turn != 1))
        def _():
            send(emb.at[pl.ds(first, T)])

        @pl.when((s >= 10) & (turn != 0))
        def _():
            send(lay.at[pl.ds(first - TAIL, T)])

    def scatter(turn, carry):
        ch = jnp.maximum(turn - 1, 0)

        @pl.when(turn == 1)
        def _():
            copies_wait(lay.at[pl.ds(0, LAY)], lay_sem)

        for kc in range(3):
            a, b, e = axes(kc)
            pos = kc * (WC) + ch * T
            far = flip(me, a)

            def share_step(j, carry):
                near = (j // 2) * DIM[b] + (j % 2) * DIM[e]
                for to in range(2):
                    s = (1 - bit(me, a)) * DIM[a] + near + to
                    send_raw(s, pos, raw.at[kc, ch, core, j], far - core + to, raw_recv.at[kc, ch], turn)
                s = bit(me, a) * DIM[a] + near + 1 - core
                send_raw(s, pos, raw.at[kc, ch, 2, j], me + 1 - 2 * core, raw_recv.at[kc, ch], turn)
                return carry

            lax.fori_loop(0, 4, share_step, 0)
        return carry

    lax.fori_loop(0, NC + 1, scatter, 0)

    def first_sum(ch, carry):
        for kc in range(3):
            a, b, e = axes(kc)
            pos = kc * (WC) + ch * T
            mine = [bit(me, a) * DIM[a] + (j // 2) * DIM[b] + (j % 2) * DIM[e] + core for j in range(4)]
            for j in range(4):
                first = start_of(mine[j]) + pos

                @pl.when(mine[j] < 10)
                def _():
                    pltpu.make_async_copy(emb.at[pl.ds(first, T)], own.at[j], own_sem.at[j]).start()

                @pl.when(mine[j] >= 10)
                def _():
                    own[j] = lay[pl.ds(first - TAIL, T)]

            copies_wait(raw.at[kc, ch], raw_recv.at[kc, ch])
            for j in range(4):
                @pl.when(mine[j] < 10)
                def _():
                    copies_wait(own.at[j], own_sem.at[j])

            def sum_step(n, carry):
                j = (n // 2 + 1 - bit(me, b)) % 2 * 2 + n % 2

                def tile_step(t, carry):
                    i = pl.ds(t * STEP, STEP)
                    acc[kc, ch, pl.ds(j * T + t * STEP, STEP)] = (
                        (own[j, i].astype(jnp.float32) + raw[kc, ch, 2, j, i].astype(jnp.float32))
                        + (raw[kc, ch, 0, j, i].astype(jnp.float32) + raw[kc, ch, 1, j, i].astype(jnp.float32)))
                    return carry

                lax.fori_loop(0, T // STEP, tile_step, 0)
                return carry

            lax.fori_loop(0, 4, sum_step, 0)
            pltpu.make_async_remote_copy(
                src_ref=acc.at[kc, ch, pl.ds(2 * (1 - bit(me, b)) * T, 2 * T)], dst_ref=recv2.at[pl.ds((kc * NC + ch) * 2 * T, 2 * T)],
                send_sem=s2_send, recv_sem=s2_recv.at[kc, ch], device_id=(flip(me, b),), device_id_type=MESH).start()
        return carry

    lax.fori_loop(0, NC, first_sum, 0)

    def second_sum(ch, carry):
        for kc in range(3):
            a, b, e = axes(kc)
            slot = (kc * NC + ch) * 2 * T
            copies_wait(recv2.at[pl.ds(slot, 2 * T)], s2_recv.at[kc, ch])
            for n in range(2):
                je = (1 - bit(me, e)) if n == 0 else bit(me, e)
                j = 2 * bit(me, b) + je

                def tile_step(t, carry):
                    i = pl.ds(t * STEP, STEP)
                    at = pl.ds(j * T + t * STEP, STEP)
                    acc[kc, ch, at] = acc[kc, ch, at] + recv2[pl.ds(slot + je * T + t * STEP, STEP)]
                    return carry

                lax.fori_loop(0, T // STEP, tile_step, 0)
            pltpu.make_async_remote_copy(
                src_ref=acc.at[kc, ch, pl.ds((2 * bit(me, b) + 1 - bit(me, e)) * T, T)], dst_ref=recv3.at[kc, ch],
                send_sem=s3_send, recv_sem=s3_recv.at[kc, ch], device_id=(flip(me, e),), device_id_type=MESH).start()
        return carry

    lax.fori_loop(0, NC, second_sum, 0)

    def third_sum(ch, carry):
        for kc in range(3):
            a, b, e = axes(kc)
            copies_wait(recv3.at[kc, ch], s3_recv.at[kc, ch])
            j = 2 * bit(me, b) + bit(me, e)

            def tile_step(t, carry):
                i = pl.ds(t * STEP, STEP)
                recv2[pl.ds((kc * NC + ch) * T + t * STEP, STEP)] = (acc[kc, ch, pl.ds(j * T + t * STEP, STEP)] + recv3[kc, ch, i]) * 0.0625
                return carry

            lax.fori_loop(0, T // STEP, tile_step, 0)
        return carry

    lax.fori_loop(0, NC, third_sum, 0)

    base = HEAD - (SHARE * me - start_of(me))
    walk_units(me, base, True, *[functools.partial(fn, recv2, flat, tmp) for fn in (rows9_to_flat, gate_to_flat, q_to_flat, kv_to_flat, copy_to_flat)])

    store = pltpu.make_async_copy(flat.at[pl.ds(0, EXT * ROWS)], flat_out, o_sem)
    store.start()

    def square_step(t, total):
        for n in range(15):
            x = flat[pl.ds((HEAD + t * 15 + n) * ROWS, ROWS), :]
            total = total + x * x
        return total

    part[me] = lax.fori_loop(0, SHARE // 15, square_step, jnp.zeros(TILE, jnp.float32))
    for step in range(1, 16):
        pltpu.make_async_remote_copy(
            src_ref=part.at[me], dst_ref=part.at[me], send_sem=n_send, recv_sem=n_recv,
            device_id=(lax.rem(me + step, 16),), device_id_type=MESH).start()
    copies_wait(part.at[pl.ds(0, 15)], n_recv)
    norm_out[...] = jnp.sum(part[...], axis=0)
    copies_wait(part.at[pl.ds(0, 15)], n_send)
    copies_wait(raw, raw_send)
    copies_wait(recv2, s2_send)
    copies_wait(recv3, s3_send)
    for copy in heads:
        copy.wait()
    store.wait()


def update_kernel(flat_in, norm_in, head, mom, var, mas, hyper,
                  gathered, m, v, p,
                  g, tmp, in_sems, send_sem, recv_sems, pair_recv):
    me = lax.axis_index("dp")
    core = me % 2
    loads = []
    for n, (src, dst) in enumerate(((mom, m), (var, v), (mas, p))):
        loads.append(pltpu.make_async_copy(src, dst.at[pl.ds(HEAD * ROWS, SHARE * ROWS)], in_sems.at[n]))
        loads.append(pltpu.make_async_copy(head.at[n], dst.at[pl.ds(0, HEAD * ROWS)], in_sems.at[n + 3]))
    loads.append(pltpu.make_async_copy(flat_in, g, in_sems.at[6]))
    for copy in loads:
        copy.start()

    def full(x):
        return jnp.full(TILE, x, jnp.float32)

    def power7(x):
        x2 = x * x
        return x2 * x2 * x2 * x

    total = full(jnp.sum(norm_in[...]))
    rate, b1, b2, decay, limit = (full(hyper[n]) for n in range(5))
    clip = jnp.minimum(1.0, limit / (jnp.sqrt(total) + CLIP_EPS))
    a1 = (1.0 - b1) * clip
    a2 = (1.0 - b2) * (clip * clip)
    fix1 = 1.0 / (1.0 - power7(b1))
    fix2 = 1.0 / (1.0 - power7(b2))
    for copy in loads:
        copy.wait()

    def update(t, carry):
        for n in range(6):
            tile = t * 6 + n
            i = pl.ds(tile * ROWS, ROWS)
            gt, pt = g[i, :], p[i, :]
            mt = b1 * m[i, :] + (1.0 - b1) * (gt * clip)
            h = gt * clip
            vt = b2 * v[i, :] + (1.0 - b2) * (h * h)
            has_decay = SHARE * me - HEAD + tile < 14130
            u = (mt * fix1) / (jnp.sqrt(vt * fix2) + ADAM_EPS) + jnp.where(has_decay, decay, 0.0) * pt
            m[i, :] = mt
            v[i, :] = vt
            p[i, :] = pt - rate * u
        return carry

    lax.fori_loop(0, EXT // 6, update, 0)
    base = HEAD - (SHARE * me - start_of(me))
    stage = gathered.at[pl.ds(me * PUB, PUB)]
    walk_units(me, base, False, *[functools.partial(fn, stage, p, tmp) for fn in (rows9_to_tiles, gate_to_tiles, q_to_tiles, kv_to_tiles, copy_to_tiles)])

    pair = me + 1 - 2 * core

    def send(src, owner, kc, target, recv):
        pltpu.make_async_remote_copy(
            src_ref=src, dst_ref=gathered.at[pl.ds(owner * PUB + kc * PC, PC)], send_sem=send_sem, recv_sem=recv,
            device_id=(target,), device_id_type=MESH).start()

    for hop in range(3):
        for kc in range(3):
            dim = (kc + hop) % 3
            send(stage.at[pl.ds(kc * PC, PC)], me, kc, flip(me, dim), recv_sems.at[kc, (0, 1, 3)[hop]])
    for kc in range(3):
        send(stage.at[pl.ds(kc * PC, PC)], me, kc, pair, pair_recv)
    for piece in range(7):
        for kc in range(3):
            a, b, e = axes(kc)
            n = piece + 1
            owner = me
            for pos, dim in enumerate((a, b, e)):
                if (n >> pos) & 1:
                    owner = flip(owner, dim)
            block = gathered.at[pl.ds(owner * PUB + kc * PC, PC)]
            copies_wait(block, recv_sems.at[kc, piece])
            if n == 1:
                send(block, owner, kc, flip(me, b), recv_sems.at[kc, 2])
            if n < 4:
                send(block, owner, kc, flip(me, e), recv_sems.at[kc, n + 3])
            send(block, owner, kc, pair, pair_recv)
    copies_wait(gathered.at[pl.ds(0, 8 * PUB)], pair_recv)
    copies_wait(gathered.at[pl.ds(0, 15 * PUB)], send_sem)


def finish_kernel(gathered, m, v, p, emb, q, k, v_out, out, gate, up, down, norm, mom_out, var_out, mas_out, sem, state_sem):
    starts = [9 * (SHARE * s // 9) - {13: 18, 14: 9}.get(s, 0) for s in range(16)] + [TAIL + LAY]
    state = [pltpu.make_async_copy(src.at[pl.ds(HEAD * ROWS, SHARE * ROWS)], dst, state_sem.at[n])
             for n, (src, dst) in enumerate(((m, mom_out), (v, var_out), (p, mas_out)))]
    for copy in state:
        copy.start()
    for dst, first, n, size in ((emb, 0, EMB, 1), (q, TAIL + OFF_Q, 54, 4), (k, TAIL + OFF_K, 54, 1), (v_out, TAIL + OFF_V, 54, 1),
                                (out, TAIL + OFF_O, 216, 1), (gate, TAIL + OFF_G, 54, 27), (up, TAIL + OFF_U, 54, 27),
                                (down, TAIL + OFF_D, 1458, 1), (norm, TAIL + OFF_N, 30, 1)):
        for s in range(16):
            lo, hi = max(starts[s], first), min(starts[s + 1], first + n * size)
            if lo >= hi:
                continue
            src = s * PUB + lo - starts[s]
            if len(dst.shape) == 3:
                pltpu.make_async_copy(gathered.at[pl.ds(src, hi - lo)], dst.at[pl.ds(lo - first, hi - lo)], sem).start()
                continue
            unit = (lo - first) // size

            def step(i, carry, dst=dst, src=src, unit=unit, size=size):
                l, rb = (unit + i) // 9, lax.rem(unit + i, 9)
                pltpu.make_async_copy(gathered.at[pl.ds(src + i * size, size)], dst.at[l, :, rb], sem).start()
                return carry

            lax.fori_loop(0, (hi - lo) // size, step, 0)
    copies_wait(gathered.at[pl.ds(0, TAIL + LAY)], sem)
    for copy in state:
        copy.wait()


ANY = pl.BlockSpec(memory_space=pl.ANY)
VM = pl.BlockSpec(memory_space=pltpu.VMEM)
DMA = pltpu.SemaphoreType.DMA


def tiled(x):
    rows, cols = x.shape[-2:]
    x = x.reshape(x.shape[:-2] + (rows // ROWS, ROWS, cols // LANES, LANES))
    return jnp.swapaxes(x, -3, -2)


def solution(mesh):
    def local_update(*arrays):
        emb, q, k, v, out, gate, up, down, norms, qk = [a[0] for a in arrays[:GRAD_COUNT]]
        mom, var, mas, hyper = arrays[GRAD_COUNT:]
        emb_t = tiled(emb).reshape(EMB, ROWS, LANES)
        q, k, v, gate, up = [tiled(jnp.swapaxes(x, 1, 2)) for x in (q, k, v, gate, up)]
        out_t, down_t = tiled(out).reshape(216, ROWS, LANES), tiled(down).reshape(1458, ROWS, LANES)
        norm = jnp.concatenate([norms.reshape(-1), qk.reshape(-1)]).reshape(30, ROWS, LANES)
        state = [x.reshape(SHARE, ROWS, LANES) for x in (mom, var, mas)]

        flat, total, head = pl.pallas_call(
            reduce_kernel,
            out_shape=(jax.ShapeDtypeStruct((EXT * ROWS, 128), jnp.float32), jax.ShapeDtypeStruct(TILE, jnp.float32),
                       jax.ShapeDtypeStruct((3, HEAD, ROWS, LANES), jnp.float32)),
            in_specs=[ANY] * 12,
            out_specs=(ANY, VM, ANY),
            scratch_shapes=[
                pltpu.VMEM((LAYP, ROWS, LANES), jnp.bfloat16),
                pltpu.VMEM((3, NC, 3, 4, T, ROWS, LANES), jnp.bfloat16),
                pltpu.VMEM((4, T, ROWS, LANES), jnp.bfloat16),
                pltpu.VMEM((3, NC, 4 * T, ROWS, LANES), jnp.float32),
                pltpu.VMEM((2 * WIN, ROWS, LANES), jnp.float32),
                pltpu.VMEM((3, NC, T, ROWS, LANES), jnp.float32),
                pltpu.VMEM(((HEAD + WIN) * ROWS, 128), jnp.float32),
                pltpu.VMEM((2, LANES, LANES), jnp.float32),
                pltpu.VMEM((16, ROWS, LANES), jnp.float32),
                DMA, DMA((2, 3)), DMA((4,)), DMA, DMA((3, NC)), DMA, DMA((3, NC)), DMA, DMA((3, NC)), DMA, DMA, DMA,
            ],
            compiler_params=pltpu.CompilerParams(has_side_effects=True, vmem_limit_bytes=67043328),
            name="reduce",
        )(emb_t, q, k, v, out_t, gate, up, down_t, norm, *state)

        rows = [x.reshape(SHARE * ROWS, 128) for x in (mom, var, mas)]
        held = [pltpu.VMEM((16 * PUB, ROWS, LANES), jnp.bfloat16)] + [pltpu.VMEM((EXT * ROWS, 128), jnp.float32)] * 3
        kept = pl.pallas_call(
            update_kernel,
            out_shape=tuple(held),
            in_specs=[ANY, VM] + [ANY] * 4 + [pl.BlockSpec(memory_space=pltpu.SMEM)],
            out_specs=(VM,) * 4,
            scratch_shapes=[
                pltpu.VMEM((EXT * ROWS, 128), jnp.float32), pltpu.VMEM((2, LANES, LANES), jnp.float32),
                DMA((7,)), DMA, DMA((3, 7)), DMA,
            ],
            compiler_params=pltpu.CompilerParams(has_side_effects=True, vmem_limit_bytes=SMALL),
            name="update",
        )(flat, total, head.reshape(3, HEAD * ROWS, 128), *rows, hyper)

        like = [emb_t, q, k, v, out_t, gate, up, down_t, norm] + rows
        emb2, q2, k2, v2, out2, gate2, up2, down2, norm2, *state2 = pl.pallas_call(
            finish_kernel,
            out_shape=tuple(jax.ShapeDtypeStruct(x.shape, x.dtype) for x in like),
            in_specs=[VM] * 4,
            out_specs=(ANY,) * 12,
            scratch_shapes=[DMA, DMA((3,))],
            compiler_params=pltpu.CompilerParams(vmem_limit_bytes=SMALL),
            name="finish",
        )(*[pltpu.with_memory_space_constraint(x, pltpu.VMEM) for x in kept])

        def matrices(x):
            return jnp.swapaxes(x, 2, 3).reshape(6, -1, 1152)

        def columns(x):
            return jnp.swapaxes(matrices(x), 1, 2)

        flat_norm = norm2.reshape(-1)
        cut = norms.size
        params = (jnp.swapaxes(emb2.reshape(1024, 9, ROWS, LANES), 1, 2).reshape(emb.shape),
                  columns(q2), columns(k2), columns(v2), matrices(out2.reshape(6, 4, 9, ROWS, LANES)), columns(gate2), columns(up2),
                  matrices(down2.reshape(6, 27, 9, ROWS, LANES)), flat_norm[:cut].reshape(norms.shape), flat_norm[cut:].reshape(qk.shape))
        return params + tuple(x.reshape(-1) for x in state2)

    in_specs = tuple([P("dp")] * GRAD_COUNT + [P("dp"), P("dp"), P("dp"), P()])
    out_specs = tuple([P()] * GRAD_COUNT + [P("dp"), P("dp"), P("dp")])
    return jax.shard_map(local_update, mesh=mesh, in_specs=in_specs, out_specs=out_specs, check_vma=False)
```

time: 1180 us -> 350 us (0.30)
  waiting for transfers between devices: 462 us -> 0 us
  local copies, waits for them, and re-layouts: 393 us -> 4.3 us
  Pallas kernels: 0 us -> 339 us
  other arithmetic: 251 us -> 0.63 us
  blocking collectives: 34.6 us -> 0 us
  between operations: 21.2 us -> 0.67 us
    all_to_all x1 -> x0, waiting for transfers between devices: 345 us -> none  [local_update(): received = lax.all_to_all(local_vec, 'dp', 0, 0, tiled=True)]
    pallas_call x0 -> x3, Pallas kernels: none -> 339 us  [the longest x1 213 us: local_update(): pl.pallas_call(reduce_kernel, out_shape=(jax.ShapeDtypeStruct((EXT * ROWS...]
    unnamed x44 -> x1, local copies, waits for them, and re-layouts: 190 us -> 0.7 us
    all_to_all x1 -> x0, other arithmetic: 174 us -> none  [local_update(): received = lax.all_to_all(local_vec, 'dp', 0, 0, tiled=True)]
    reshape x18 -> x2, local copies, waits for them, and re-layouts: 144 us -> 1.25 us  [the longest x1 0.65 us: local_update(): flat_norm[:cut].reshape(norms.shape)]
    all_gather x1 -> x0, waiting for transfers between devices: 118 us -> none  [local_update(): full_vec = lax.all_gather(new_master.astype(jnp.bfloat16), 'dp', tiled=True)]
    reduce_sum x2 -> x0, other arithmetic: 64.9 us -> none  [the longest x1 63.4 us: local_update(): grad_part = jnp.sum(received, axis=0, dtype=jnp.float32) / group_size]
    psum x1 -> x0, blocking collectives: 34.6 us -> none  [local_update(): square_sum = lax.psum(jnp.sum(grad_part * grad_part), 'dp')]
  transfers between devices with their start and end apart: 2 -> 0, of which waited for: 2 -> 0; matrix products, arithmetic and copies ran while one was open for 0% -> 0% of each run, Pallas kernels for 0% -> 0%
where the time goes in v1:
time: 350 us; the launch traced here: 345 us
  Pallas kernels  339 us (97%)
  local copies, waits for them, and re-layouts  4.3 us (1%)
    pallas_call x1, Pallas kernels, local_update(): pl.pallas_call(reduce_kernel, out_shape=(jax.ShapeDtypeStruct((EXT * ROWS...  213 us
    pallas_call x1, Pallas kernels, local_update(): pl.pallas_call(update_kernel, out_shape=tuple(held), in_specs=[ANY, VM] +...  113 us
    pallas_call x1, Pallas kernels, local_update(): pl.pallas_call(finish_kernel, out_shape=tuple((jax.ShapeDtypeStruct(x.sha...  13.2 us

profile of v1, /device:TPU:0, one launch (start us, length us, event | category | flops | bytes accessed | tf_op | source)
XLA Modules:
  0.0 344.7 jit_solution(11664924637500066365)
XLA Ops:
  0.6 0.7 copy.27
  1.3 0.8 reshape_squeeze.18
  2.2 0.6 maximum_bitcast_fusion.norm
  2.8 212.7 %reduce.1 = (f32[7248,128]{1,0:T(8,128)}, f32[8,128]{1,0:T(8,128)}, f32[3,21,8,128]{3,2,1,0:T(8,128)}) custom-call(bf16[9216,8,128]{2,1,0:T(8,128)(2,1)} %bitcast.104, bf16[6,4,9,8,128]{4,3,2,1,0:T(8,128)(2,1)} %bitcast.114, bf16[6,1,9,8,128]{4,3,2,1,0:T(8,128)(2,1)} %bitcast.117, bf16[6,1,9,8,128]{4,3,2,1,0:T(8,128)(2,1)} %bitcast.118, ...), custom_call_target="tpu_custom_call" | custom-call | tf_op jit(solution)/shard_map/reduce/pallas_call | solution.py:509
  215.6 113.1 %update.1 = (bf16[14400,8,128]{2,1,0:T(8,128)(2,1)S(1)}, f32[7248,128]{1,0:T(8,128)S(1)}, f32[7248,128]{1,0:T(8,128)S(1)}, f32[7248,128]{1,0:T(8,128)S(1)}) custom-call(f32[7248,128]{1,0:T(8,128)} %get-tuple-element.32.flat_in, f32[8,128]{1,0:T(8,128)} %get-tuple-element.33.norm_in, f32[3,168,128]{2,1,0:T(8,128)} %bitcast.116, f32[7080,128]{1,0:T(8,128)} %bitcast.106, ...), custom_call_target="tpu_custom_call" | custom-call | tf_op jit(solution)/shard_map/update/pallas_call | solution.py:533
  328.7 13.2 %finish.1 = (bf16[9216,8,128]{2,1,0:T(8,128)(2,1)}, bf16[6,4,9,8,128]{4,3,2,1,0:T(8,128)(2,1)}, bf16[6,1,9,8,128]{4,3,2,1,0:T(8,128)(2,1)}, bf16[6,1,9,8,128]{4,...) custom-call(bf16[14400,8,128]{2,1,0:T(8,128)(2,1)S(1)} %get-tuple-el, ...), custom_call_target="tpu_custom_call" | custom-call | tf_op jit(solution)/shard_map/finish/pallas_call | solution.py:547
  341.9 0.7 slice.9
  342.6 0.8 slice.8
  343.4 0.6 reshape.154
  344.1 0.6 reshape.155

commit v2 on v0

v2 whole, which is shorter than its diff:
```python
import functools
import jax
import jax.numpy as jnp
from jax import lax
from jax.experimental import pallas as pl
from jax.experimental.pallas import tpu as pltpu
from jax.sharding import PartitionSpec as P

ADAM_EPS = 1e-8
CLIP_EPS = 1e-6
GRAD_COUNT = 10
MESH = pl.DeviceIdType.MESH
F32, BF16 = jnp.float32, jnp.bfloat16

ROWS, LANES = 8, 128
TILE = (ROWS, LANES)
DEVICES = 16
SHARE = 885
WIN = 891
WIDE = 918
CUT = (14, 13)
NC = 9
T = 33
STEP = 11
MINI = 9
EMB = 9216
TAIL = 8847
LAY = 5313
LAYP = LAY + MINI
HALF = 2367
HEAD = 21
PUB = 900
NA = 3
PC = 100
EXT = HEAD + SHARE
OFF_Q, OFF_K, OFF_V, OFF_O = 369, 585, 639, 693
OFF_G, OFF_U, OFF_D, OFF_N = 909, 2367, 3825, 5283
DIM = (2, 4, 8)
SHIFT = 88
GRANT = 26300000
RAW_END = 12 * WIN
OWN_AT = RAW_END
RAW_M = OWN_AT + 12 * T
OWN_M = RAW_M + 9 * MINI
STAGE_AT = OWN_M + 3 * MINI


def start_of(s):
    return 9 * ((SHARE * s) // 9) - jnp.where(s == 13, 18, 0) - jnp.where(s == 14, 9, 0)


def axes(colour):
    return [(colour + n) % 3 for n in range(3)]


def bit(d, dim):
    return (d // DIM[dim]) % 2


def flip(d, dim):
    return d + DIM[dim] * (1 - 2 * bit(d, dim))


def copies_wait(ref, sem):
    pltpu.make_async_copy(ref, ref, sem).wait()


def put(src, dst, send_sem, recv_sem, target):
    copy = pltpu.make_async_remote_copy(
        src_ref=src, dst_ref=dst, send_sem=send_sem, recv_sem=recv_sem, device_id=(target,), device_id_type=MESH)
    copy.start()
    return copy


def loop(lo, hi, fn):
    def step(i, carry):
        fn(i)
        return carry
    lax.fori_loop(lo, hi, step, 0)


def lanes():
    return lax.broadcasted_iota(jnp.int32, TILE, 1)


def gate_segments():
    rows = []
    for kap in range(27):
        pieces, f = [], LANES * kap
        while f < LANES * (kap + 1):
            i, c = f // 216, f % 216
            pieces.append((f - LANES * kap, i, c // LANES))
            f = min(LANES * (kap + 1), 216 * i + (LANES if c < LANES else 216))
        rows.append(pieces)
    return rows


def gate_inverse():
    table = {}
    for kap, pieces in enumerate(gate_segments()):
        ends = [lo for lo, _, _ in pieces[1:]] + [LANES]
        for (lo, i, half), hi in zip(pieces, ends):
            table.setdefault((i, half), []).append((lo, hi, kap))
    return table


def swap_groups(xs, width):
    ids = lanes() // width
    xs, step = list(xs), 1
    while step < len(xs):
        high = (ids // step) % 2 == 1
        for n in range(len(xs)):
            if not n & step:
                lo, hi = xs[n], xs[n + step]
                xs[n] = jnp.where(high, pltpu.roll(hi, width * step, 1), lo)
                xs[n + step] = jnp.where(high, hi, pltpu.roll(lo, LANES - width * step, 1))
        step = 2 * step
    return xs


def turned(win, o):
    return win[pl.ds(o, 16)].reshape(LANES, LANES).T


def rows9_to_flat(win, flat, tmp, o, f):
    for ct in range(9):
        flat[pl.ds(f * ROWS + ct, ROWS, 9), :] = win[o + ct]


def gate_to_flat(win, flat, tmp, o, f):
    for half in range(2):
        tmp[half] = turned(win, o + 16 * half)
    ids = lanes()
    rolled = {}
    for i in range(16):
        for half in range(2):
            rolled[i, half] = pltpu.roll(tmp[half, pl.ds(i, ROWS, 16), :], (SHIFT * i) % LANES, 1)
    for kap, pieces in enumerate(gate_segments()):
        val = None
        for lo, i, half in pieces:
            val = rolled[i, half] if val is None else jnp.where(ids >= lo, rolled[i, half], val)
        flat[pl.ds(f * ROWS + kap, ROWS, 27), :] = val


def q_to_flat(win, flat, tmp, o, f):
    tmp[0] = turned(win, o)
    for kb in range(4):
        xs = swap_groups([tmp[0, pl.ds(32 * kb + i, ROWS, 4), :] for i in range(4)], 32)
        for u in range(4):
            flat[pl.ds((f + 4 * u + kb) * ROWS, ROWS), :] = xs[u]


def kv_to_flat(win, flat, tmp, o, f):
    tmp[0] = turned(win, o)
    xs = swap_groups([tmp[0, pl.ds(i, ROWS, 16), :] for i in range(16)], ROWS)
    for u in range(16):
        flat[pl.ds((f + u) * ROWS, ROWS), :] = xs[u]


def copy_to_flat(win, flat, tmp, o, f):
    flat[pl.ds(f * ROWS, ROWS), :] = win[o]


def rows9_to_tiles(stage, flat, tmp, o, f):
    for ct in range(9):
        stage[o + ct] = flat[pl.ds(f * ROWS + ct, ROWS, 9), :].astype(BF16)


def gate_to_tiles(stage, flat, tmp, o, f):
    ids = lanes()
    rows = [flat[pl.ds(f * ROWS + kap, ROWS, 27), :] for kap in range(27)]
    for (i, half), pieces in gate_inverse().items():
        val = rows[pieces[0][2]]
        for lo, hi, kap in pieces[1:]:
            val = jnp.where((ids >= lo) & (ids < hi), rows[kap], val)
        tmp[half, pl.ds(i, ROWS, 16), :] = pltpu.roll(val, (LANES - SHIFT * i) % LANES, 1)
    stage[pl.ds(o, 16)] = tmp[0].T.reshape(16, ROWS, LANES).astype(BF16)
    stage[pl.ds(o + 16, 11)] = tmp[1].T[:SHIFT].reshape(11, ROWS, LANES).astype(BF16)


def q_to_tiles(stage, flat, tmp, o, f):
    for kb in range(4):
        xs = swap_groups([flat[pl.ds((f + 4 * u + kb) * ROWS, ROWS), :] for u in range(4)], 32)
        for i in range(4):
            tmp[0, pl.ds(32 * kb + i, ROWS, 4), :] = xs[i]
    stage[pl.ds(o, 16)] = tmp[0].T.reshape(16, ROWS, LANES).astype(BF16)


def kv_to_tiles(stage, flat, tmp, o, f):
    xs = swap_groups([flat[pl.ds((f + u) * ROWS, ROWS), :] for u in range(16)], ROWS)
    for i in range(16):
        tmp[0, pl.ds(i, ROWS, 16), :] = xs[i]
    stage[pl.ds(o, 16)] = tmp[0].T.reshape(16, ROWS, LANES).astype(BF16)


def copy_to_tiles(stage, flat, tmp, o, f):
    stage[o] = flat[pl.ds(f * ROWS, ROWS), :].astype(BF16)


TO_FLAT = (rows9_to_flat, gate_to_flat, q_to_flat, kv_to_flat, copy_to_flat)
TO_TILES = (rows9_to_tiles, gate_to_tiles, q_to_tiles, kv_to_tiles, copy_to_tiles)


def walk_units(me, wide, lo, hi, fns, run):
    def pick(table):
        return sum(jnp.where(me == d, n, 0) for d, n in table.items())
    rows9, gate, q, kv, one = fns
    ends = (SHARE * (me + 1) + (8 if wide else 0)) // 9 - (SHARE * me) // 9
    first = jnp.where(me < 10, ends, pick({10: 41, 11: 3, 15: 95}))
    n_gate = pick({11: 32, 12: 33 if wide else 32, 13: 34 if wide else 33, 14: 11})
    second = pick({10: 22 if wide else 21, 14: 67})
    pos = 0
    for count, size, fn, over in ((first, 9, rows9, 0), (pick({10: 14}), 16, q, pick({10: 8})), (pick({10: 7}), 16, kv, pick({10: 4})),
                                  (n_gate, 27, gate, 0), (second, 9, rows9, 0), (pick({15: 30}), 1, one, 0)):
        def done(x):
            return jnp.minimum(jnp.maximum(x - pos + (0 if wide else size - 1), 0) // size, count)

        loop(done(lo), done(hi), lambda u, pos=pos, size=size, fn=fn: run(fn, pos + u * size))
        pos = pos + count * size - over


def step_kernel(emb, q, k, v, out, gate, up, down, norm, mom, var, mas, hyper,
                full, m_buf, v_buf, p_buf, lay,
                acc, buf, recv3, tmp, part, acc_m, recv2_m, recv3_m,
                lay_sem, state_sem, head_sems, own_sem, raw_send, raw_recv, s2_send, s2_recv, s3_send, s3_recv, n_send, n_recv,
                m_raw_send, m_raw_recv, m_own, m_send, m_recv, a_send, a_recv, pair_recv):
    me = lax.axis_index("dp")
    core = me % 2
    pair = me + 1 - 2 * core
    flat = buf.reshape(2 * WIDE * ROWS, LANES)

    state = ((mom, m_buf), (var, v_buf), (mas, p_buf))
    loads = [pltpu.make_async_copy(src, dst.at[pl.ds(HEAD * ROWS, SHARE * ROWS)], state_sem.at[n]) for n, (src, dst) in enumerate(state)]
    for copy in loads:
        copy.start()
    heads = [put(src.at[pl.ds((SHARE - HEAD) * ROWS, HEAD * ROWS)], dst.at[pl.ds(0, HEAD * ROWS)], head_sems.at[0, n], head_sems.at[1, n],
                 lax.rem(me + 1, DEVICES)) for n, (src, dst) in enumerate(state)]

    def raw_at(kc, ch, src, j):
        return full.at[pl.ds(((kc * NC + ch) * 12 + src * 4 + j) * T, T)]

    def share_tiles(s, pos, n, fn):
        first = start_of(s) + pos

        @pl.when(s < 10)
        def _():
            fn(emb.at[pl.ds(first, n)])

        @pl.when(s >= 10)
        def _():
            fn(lay.at[pl.ds(first - TAIL, n)])

    def scatter(ch, with_emb, with_lay):
        def one(s, kc, src, j, target):
            @pl.when(jnp.where(s < 10, with_emb, with_lay) == 1)
            def _():
                share_tiles(s, (ch * 3 + kc) * T, T, lambda ref: put(ref, raw_at(kc, ch, src, j), raw_send, raw_recv.at[kc, ch], target))

        for kc in range(3):
            a, b, e = axes(kc)
            far = flip(me, a)

            def share_step(j):
                near = (j // 2) * DIM[b] + (j % 2) * DIM[e]
                for to in range(2):
                    one((1 - bit(me, a)) * DIM[a] + near + to, kc, core, j, far - core + to)
                one(bit(me, a) * DIM[a] + near + 1 - core, kc, 2, j, pair)

            loop(0, 4, share_step)

    loop(0, 3, lambda ch: scatter(ch, 1, 0))
    for lo, whole, split in ((0, ((emb.at[pl.ds(TAIL, OFF_Q)], 0), (out, OFF_O)), ((q, OFF_Q, 4), (k, OFF_K, 1), (v, OFF_V, 1), (gate, OFF_G, 27))),
                             (HALF, ((down, OFF_D), (norm, OFF_N)), ((up, OFF_U, 27),))):
        n = HALF if lo == 0 else LAY - HALF
        stage = full.at[pl.ds(STAGE_AT, n)]
        for src, off in whole:
            pltpu.make_async_copy(src, full.at[pl.ds(STAGE_AT + off - lo, src.shape[0])], lay_sem.at[0]).start()

        def load(i):
            for src, off, size in split:
                pltpu.make_async_copy(src.at[i // 9, :, lax.rem(i, 9)], full.at[pl.ds(STAGE_AT + off - lo + i * size, size)], lay_sem.at[0]).start()

        loop(0, 54, load)
        copies_wait(stage, lay_sem.at[0])
        save = pltpu.make_async_copy(stage, lay.at[pl.ds(lo, n)], lay_sem.at[1])
        save.start()
        save.wait()
    loop(0, NC, lambda ch: scatter(ch, jnp.where(ch < 3, 0, 1), 1))

    cut = jnp.where(core == 0, *CUT)

    def extra_at(kc):
        return WIN + kc * MINI

    def extra_sends(fn):
        for kc in range(3):
            for to, s in enumerate(CUT):
                far = bit(me, kc) != bit(s, kc)

                @pl.when(far | (core != to))
                def _():
                    fn(kc, to, s, far)

    def extra_send(kc, to, s, far):
        put(lay.at[pl.ds(start_of(s) - TAIL + extra_at(kc), MINI)],
            full.at[pl.ds(RAW_M + (kc * 3 + jnp.where(far, core, 2)) * MINI, MINI)], m_raw_send.at[kc, to], m_raw_recv.at[kc],
            jnp.where(far, flip(me, kc), me) - core + to)

    extra_sends(extra_send)

    def fetch(ch, kc):
        a, b, e = axes(kc)
        for j in range(4):
            s = bit(me, a) * DIM[a] + (j // 2) * DIM[b] + (j % 2) * DIM[e] + core
            share_tiles(s, (ch * 3 + kc) * T, T,
                        lambda ref: pltpu.make_async_copy(ref, full.at[pl.ds(OWN_AT + (kc * 4 + j) * T, T)], own_sem.at[kc]).start())

    for kc in range(3):
        fetch(0, kc)

    def first_sum(ch):
        for kc in range(3):
            a, b, e = axes(kc)
            copies_wait(full.at[pl.ds((kc * NC + ch) * 12 * T, 12 * T)], raw_recv.at[kc, ch])
            copies_wait(full.at[pl.ds(OWN_AT + kc * 4 * T, 4 * T)], own_sem.at[kc])

            def sum_step(n):
                j = (n // 2 + 1 - bit(me, b)) % 2 * 2 + n % 2

                def tile_step(t):
                    def one(at):
                        return full[pl.ds(at + t * STEP, STEP)].astype(F32)
                    raw = [one(((kc * NC + ch) * 12 + src * 4 + j) * T) for src in range(3)]
                    acc[kc, ch, pl.ds(j * T + t * STEP, STEP)] = (one(OWN_AT + (kc * 4 + j) * T) + raw[2]) + (raw[0] + raw[1])

                loop(0, T // STEP, tile_step)

            loop(0, 4, sum_step)
            put(acc.at[kc, ch, pl.ds(2 * (1 - bit(me, b)) * T, 2 * T)], buf.at[pl.ds((kc * NC + ch) * 2 * T, 2 * T)],
                s2_send, s2_recv.at[kc, ch], flip(me, b))

            @pl.when(ch + 1 < NC)
            def _():
                fetch(ch + 1, kc)

    loop(0, NC, first_sum)

    def near(*dims):
        same = bit(me, dims[0]) == bit(cut, dims[0])
        for dim in dims[1:]:
            same = same & (bit(me, dim) == bit(cut, dim))
        return same

    for kc in range(3):
        a, b, e = axes(kc)

        @pl.when(near(a))
        def _():
            own = full.at[pl.ds(OWN_M + kc * MINI, MINI)]
            copy = pltpu.make_async_copy(lay.at[pl.ds(start_of(cut) - TAIL + extra_at(kc), MINI)], own, m_own)
            copy.start()
            raw = [full.at[pl.ds(RAW_M + (kc * 3 + src) * MINI, MINI)] for src in range(3)]
            copies_wait(full.at[pl.ds(RAW_M + kc * 3 * MINI, 3 * MINI)], m_raw_recv.at[kc])
            copy.wait()
            acc_m[kc] = (own[...].astype(F32) + raw[2][...].astype(F32)) + (raw[0][...].astype(F32) + raw[1][...].astype(F32))

            @pl.when(bit(me, b) != bit(cut, b))
            def _():
                put(acc_m.at[kc], recv2_m.at[kc], m_send.at[kc], m_recv.at[0, kc], flip(me, b))

    def second_sum(ch):
        for kc in range(3):
            a, b, e = axes(kc)
            slot = (kc * NC + ch) * 2 * T
            copies_wait(buf.at[pl.ds(slot, 2 * T)], s2_recv.at[kc, ch])
            for je in ((1 - bit(me, e)), bit(me, e)):
                def tile_step(t):
                    at = pl.ds((2 * bit(me, b) + je) * T + t * STEP, STEP)
                    acc[kc, ch, at] = acc[kc, ch, at] + buf[pl.ds(slot + je * T + t * STEP, STEP)]

                loop(0, T // STEP, tile_step)
            put(acc.at[kc, ch, pl.ds((2 * bit(me, b) + 1 - bit(me, e)) * T, T)], recv3.at[pl.ds((ch * 3 + kc) * T, T)],
                s3_send, s3_recv.at[kc, ch], flip(me, e))

    loop(0, NC, second_sum)
    for kc in range(3):
        a, b, e = axes(kc)

        @pl.when(near(a, b))
        def _():
            copies_wait(recv2_m.at[kc], m_recv.at[0, kc])
            acc_m[kc] = acc_m[kc] + recv2_m[kc]

            @pl.when(bit(me, e) != bit(cut, e))
            def _():
                put(acc_m.at[kc], recv3_m.at[kc], m_send.at[kc], m_recv.at[1, kc], flip(me, e))

    base = HEAD - (SHARE * me - start_of(me))

    def to_flat(lo, hi):
        walk_units(me, True, lo, hi, TO_FLAT, lambda fn, o: fn(buf, flat, tmp, o, WIDE + base + o))

    def flat_rows(t):
        return pl.ds((WIDE + t) * ROWS, ROWS)

    def squares(lo, hi, total):
        def step(t, total):
            for n in range(15):
                x = flat[flat_rows(HEAD + t * 15 + n), :]
                total = total + x * x
            return total
        return lax.fori_loop(lo, hi, step, total)

    def ready(ch):
        return jnp.maximum((ch * 3 * T - 48) // 15, 0)

    def third_sum(ch, total):
        for kc in range(3):
            a, b, e = axes(kc)
            copies_wait(recv3.at[pl.ds((ch * 3 + kc) * T, T)], s3_recv.at[kc, ch])

            def tile_step(t):
                i = pl.ds((ch * 3 + kc) * T + t * STEP, STEP)
                buf[i] = (acc[kc, ch, pl.ds((2 * bit(me, b) + bit(me, e)) * T + t * STEP, STEP)] + recv3[i]) * 0.0625

            loop(0, T // STEP, tile_step)
        to_flat(ch * 3 * T, (ch + 1) * 3 * T)
        return squares(ready(ch), ready(ch + 1), total)

    total = lax.fori_loop(0, NC, third_sum, jnp.zeros(TILE, F32))

    @pl.when(me == cut)
    def _():
        for kc in range(3):
            copies_wait(recv3_m.at[kc], m_recv.at[1, kc])
            buf[pl.ds(extra_at(kc), MINI)] = (acc_m[kc] + recv3_m[kc]) * 0.0625

    to_flat(NC * 3 * T, 2 * WIDE)
    part[me] = squares(ready(NC), SHARE // 15, total)
    loop(1, DEVICES, lambda n: put(part.at[me], part.at[me], n_send, n_recv, lax.rem(me + n, DEVICES)))

    for copy in loads + heads:
        copy.wait()

    def fill(x):
        return jnp.full(TILE, x, F32)

    def power7(x):
        x2 = x * x
        return x2 * x2 * x2 * x

    rate, b1, b2, decay, limit = (fill(hyper[n]) for n in range(5))
    fix1 = 1.0 / (1.0 - power7(b1))
    fix2 = 1.0 / (1.0 - power7(b2))
    others = pl.ds(0, DEVICES - 1)
    copies_wait(part.at[others], n_recv)
    norm_sum = fill(jnp.sum(jnp.sum(part[...], axis=0)))
    clip = jnp.minimum(1.0, limit / (jnp.sqrt(norm_sum) + CLIP_EPS))

    def update(t):
        for n in range(6):
            tile = t * 6 + n
            i = pl.ds(tile * ROWS, ROWS)
            h = flat[flat_rows(tile), :] * clip
            pt = p_buf[i, :]
            mt = b1 * m_buf[i, :] + (1.0 - b1) * h
            vt = b2 * v_buf[i, :] + (1.0 - b2) * (h * h)
            has_decay = SHARE * me - HEAD + tile < TAIL + OFF_N
            u = (mt * fix1) / (jnp.sqrt(vt * fix2) + ADAM_EPS) + jnp.where(has_decay, decay, 0.0) * pt
            m_buf[i, :] = mt
            v_buf[i, :] = vt
            p_buf[i, :] = pt - rate * u

    def send(owner, c, kc, target, recv):
        block = full.at[pl.ds(owner * PUB + (c * 3 + kc) * PC, PC)]
        put(block, block, a_send, recv, target)

    mine = full.at[pl.ds(me * PUB, PUB)]

    def publish(c):
        loop(jnp.where(c == 0, 0, 9 + 50 * c), jnp.minimum(59 + 50 * c, EXT // 6), update)
        walk_units(me, False, c * 3 * PC, (c + 1) * 3 * PC, TO_TILES, lambda fn, o: fn(mine, p_buf, tmp, o, base + o))
        for hop in range(3):
            for kc in range(3):
                dim = axes(kc)[hop]
                send(me, c, kc, flip(me, dim), a_recv.at[c, kc, (0, 1, 3)[hop]])
        for kc in range(3):
            send(me, c, kc, pair, pair_recv)

    loop(0, NA, publish)

    def pass_on(level, c):
        for kc in range(3):
            a, b, e = axes(kc)
            for n in ((1,), (2, 3), (4, 5, 6, 7))[level]:
                owner = me
                for pos, dim in enumerate((a, b, e)):
                    if (n >> pos) & 1:
                        owner = flip(owner, dim)
                copies_wait(full.at[pl.ds(owner * PUB + (c * 3 + kc) * PC, PC)], a_recv.at[c, kc, n - 1])
                if level == 0:
                    send(owner, c, kc, flip(me, b), a_recv.at[c, kc, 2])
                if level < 2:
                    send(owner, c, kc, flip(me, e), a_recv.at[c, kc, n + 3])
                send(owner, c, kc, pair, pair_recv)

    for level in range(3):
        loop(0, NA, functools.partial(pass_on, level))

    copies_wait(full.at[pl.ds(0, DEVICES // 2 * PUB)], pair_recv)
    copies_wait(full.at[pl.ds(0, (DEVICES - 1) * PUB)], a_send)
    copies_wait(full.at[pl.ds(0, RAW_END)], raw_send)
    copies_wait(buf.at[pl.ds(0, 2 * WIN)], s2_send)
    copies_wait(recv3, s3_send)
    copies_wait(part.at[others], n_send)
    extra_sends(lambda kc, to, s, far: copies_wait(lay.at[pl.ds(0, MINI)], m_raw_send.at[kc, to]))
    for kc in range(3):
        a, b, e = axes(kc)

        @pl.when(near(a) & jnp.logical_not(near(a, b, e)))
        def _():
            copies_wait(acc_m.at[kc], m_send.at[kc])


def finish_kernel(gathered, m, v, p, emb, q, k, v_out, out, gate, up, down, norm, mom_out, var_out, mas_out, sem, state_sem):
    starts = [9 * (SHARE * s // 9) - {13: 18, 14: 9}.get(s, 0) for s in range(16)] + [TAIL + LAY]
    state = [pltpu.make_async_copy(src.at[pl.ds(HEAD * ROWS, SHARE * ROWS)], dst, state_sem.at[n])
             for n, (src, dst) in enumerate(((m, mom_out), (v, var_out), (p, mas_out)))]
    for copy in state:
        copy.start()
    for dst, first, n, size in ((emb, 0, EMB, 1), (q, TAIL + OFF_Q, 54, 4), (k, TAIL + OFF_K, 54, 1), (v_out, TAIL + OFF_V, 54, 1),
                                (out, TAIL + OFF_O, 216, 1), (gate, TAIL + OFF_G, 54, 27), (up, TAIL + OFF_U, 54, 27),
                                (down, TAIL + OFF_D, 1458, 1), (norm, TAIL + OFF_N, 30, 1)):
        for s in range(16):
            lo, hi = max(starts[s], first), min(starts[s + 1], first + n * size)
            if lo >= hi:
                continue
            src = s * PUB + lo - starts[s]
            if len(dst.shape) == 3:
                pltpu.make_async_copy(gathered.at[pl.ds(src, hi - lo)], dst.at[pl.ds(lo - first, hi - lo)], sem).start()
                continue
            unit = (lo - first) // size

            def step(i, carry, dst=dst, src=src, unit=unit, size=size):
                l, rb = (unit + i) // 9, lax.rem(unit + i, 9)
                pltpu.make_async_copy(gathered.at[pl.ds(src + i * size, size)], dst.at[l, :, rb], sem).start()
                return carry

            lax.fori_loop(0, (hi - lo) // size, step, 0)
    copies_wait(gathered.at[pl.ds(0, TAIL + LAY)], sem)
    for copy in state:
        copy.wait()


ANY = pl.BlockSpec(memory_space=pl.ANY)
VM = pl.BlockSpec(memory_space=pltpu.VMEM)
DMA = pltpu.SemaphoreType.DMA


def tiled(x):
    rows, cols = x.shape[-2:]
    x = x.reshape(x.shape[:-2] + (rows // ROWS, ROWS, cols // LANES, LANES))
    return jnp.swapaxes(x, -3, -2)


def flat_tiles(x):
    return tiled(x).reshape((-1,) + TILE)


def solution(mesh):
    def local_update(*arrays):
        emb, q, k, v, out, gate, up, down, norms, qk = [a[0] for a in arrays[:GRAD_COUNT]]
        *state, hyper = arrays[GRAD_COUNT:]
        q_t, k_t, v_t, gate_t, up_t = [tiled(jnp.swapaxes(x, 1, 2)) for x in (q, k, v, gate, up)]
        norm = jnp.concatenate([norms.reshape(-1), qk.reshape(-1)]).reshape((-1,) + TILE)
        rows = [x.reshape(SHARE * ROWS, LANES) for x in state]
        args = [flat_tiles(emb), q_t, k_t, v_t, flat_tiles(out), gate_t, up_t, flat_tiles(down), norm] + rows

        *kept, _ = pl.pallas_call(
            step_kernel,
            out_shape=(pltpu.VMEM((DEVICES * PUB,) + TILE, BF16),) + (pltpu.VMEM((EXT * ROWS, LANES), F32),) * 3
            + (jax.ShapeDtypeStruct((LAYP,) + TILE, BF16),),
            in_specs=[ANY] * 12 + [pl.BlockSpec(memory_space=pltpu.SMEM)],
            out_specs=(VM,) * 4 + (ANY,),
            scratch_shapes=[
                pltpu.VMEM((3, NC, 4 * T) + TILE, F32), pltpu.VMEM((2 * WIDE,) + TILE, F32), pltpu.VMEM((WIN,) + TILE, F32),
                pltpu.VMEM((2, LANES, LANES), F32), pltpu.VMEM((DEVICES,) + TILE, F32)]
            + [pltpu.VMEM((3, MINI) + TILE, F32)] * 3
            + [DMA((2,)), DMA((3,)), DMA((2, 3)), DMA((3,)), DMA, DMA((3, NC)), DMA, DMA((3, NC)), DMA, DMA((3, NC)), DMA, DMA,
               DMA((3, 2)), DMA((3,)), DMA, DMA((3,)), DMA((2, 3)), DMA, DMA((NA, 3, 7)), DMA],
            compiler_params=pltpu.CompilerParams(has_side_effects=True, vmem_limit_bytes=GRANT),
            name="step",
        )(*args, hyper)

        emb2, q2, k2, v2, out2, gate2, up2, down2, norm2, *state2 = pl.pallas_call(
            finish_kernel,
            out_shape=tuple(jax.ShapeDtypeStruct(x.shape, x.dtype) for x in args),
            in_specs=[VM] * 4,
            out_specs=(ANY,) * 12,
            scratch_shapes=[DMA, DMA((3,))],
            compiler_params=pltpu.CompilerParams(vmem_limit_bytes=GRANT),
            name="finish",
        )(*[pltpu.with_memory_space_constraint(x, pltpu.VMEM) for x in kept])

        def matrices(x, like):
            x = x.reshape(like.shape[:-2] + (-1, like.shape[-1] // LANES) + TILE)
            return jnp.swapaxes(x, -3, -2).reshape(like.shape)

        def columns(x, like):
            return jnp.swapaxes(matrices(x, jnp.swapaxes(like, 1, 2)), 1, 2)

        flat_norm = norm2.reshape(-1)
        cut = norms.size
        params = (matrices(emb2, emb), columns(q2, q), columns(k2, k), columns(v2, v), matrices(out2, out), columns(gate2, gate), columns(up2, up),
                  matrices(down2, down), flat_norm[:cut].reshape(norms.shape), flat_norm[cut:].reshape(qk.shape))
        return params + tuple(x.reshape(-1) for x in state2)

    in_specs = tuple([P("dp")] * GRAD_COUNT + [P("dp"), P("dp"), P("dp"), P()])
    out_specs = tuple([P()] * GRAD_COUNT + [P("dp"), P("dp"), P("dp")])
    return jax.shard_map(local_update, mesh=mesh, in_specs=in_specs, out_specs=out_specs, check_vma=False)
```

time: 1180 us -> 324 us (0.27); the launches traced: 1170 us -> 324 us
  waiting for transfers between devices: 462 us -> 0 us
  local copies, waits for them, and re-layouts: 393 us -> 4.3 us
  Pallas kernels: 0 us -> 318 us
  other arithmetic: 251 us -> 0.63 us
  blocking collectives: 34.6 us -> 0 us
  between operations: 21.2 us -> 0.66 us
    all_to_all x1 -> x0, waiting for transfers between devices: 345 us -> none  [local_update(): received = lax.all_to_all(local_vec, 'dp', 0, 0, tiled=True)]
    pallas_call x0 -> x2, Pallas kernels: none -> 318 us  [the longest x1 305 us: local_update(): pl.pallas_call(step_kernel, out_shape=(pltpu.VMEM((DEVICES * PUB,) + TILE...]
    unnamed x44 -> x1, local copies, waits for them, and re-layouts: 190 us -> 0.7 us
    all_to_all x1 -> x0, other arithmetic: 174 us -> none  [local_update(): received = lax.all_to_all(local_vec, 'dp', 0, 0, tiled=True)]
    reshape x18 -> x2, local copies, waits for them, and re-layouts: 144 us -> 1.25 us  [the longest x1 0.65 us: local_update(): flat_norm[:cut].reshape(norms.shape)]
    all_gather x1 -> x0, waiting for transfers between devices: 118 us -> none  [local_update(): full_vec = lax.all_gather(new_master.astype(jnp.bfloat16), 'dp', tiled=True)]
    reduce_sum x2 -> x0, other arithmetic: 64.9 us -> none  [the longest x1 63.4 us: local_update(): grad_part = jnp.sum(received, axis=0, dtype=jnp.float32) / group_size]
    psum x1 -> x0, blocking collectives: 34.6 us -> none  [local_update(): square_sum = lax.psum(jnp.sum(grad_part * grad_part), 'dp')]
  transfers between devices with their start and end apart: 2 -> 0, of which waited for: 2 -> 0; matrix products, arithmetic and copies ran while one was open for 0% -> 0% of each run, Pallas kernels for 0% -> 0%
where the time goes in v2:
time: 324 us
  Pallas kernels  318 us (98%)
  local copies, waits for them, and re-layouts  4.3 us (1%)
    pallas_call x1, Pallas kernels, local_update(): pl.pallas_call(step_kernel, out_shape=(pltpu.VMEM((DEVICES * PUB,) + TILE...  305 us
    pallas_call x1, Pallas kernels, local_update(): pl.pallas_call(finish_kernel, out_shape=tuple((jax.ShapeDtypeStruct(x.sha...  13.2 us

profile of v2, /device:TPU:0, one launch (start us, length us, event | category | flops | bytes accessed | tf_op | source)
XLA Modules:
  0.0 323.8 jit_solution(15143410738247744299)
XLA Ops:
  0.6 0.7 copy.27
  1.3 0.8 reshape_squeeze.18
  2.2 0.6 maximum_bitcast_fusion.norm
  2.8 305.0 %step.1 = (bf16[14400,8,128]{2,1,0:T(8,128)(2,1)S(1)}, f32[7248,128]{1,0:T(8,128)S(1)}, f32[7248,128]{1,0:T(8,128)S(1)}, f32[7248,128]{1,0:T(8,128)S(1)}, bf16[5322,8,128]{2,1,0:T(8,128)(2,1)}) custom-call(bf16[9216,8,128]{2,1,0:T(8,128)(2,1)} %bitcast.100, bf16[6,4,9,8,128]{4,3,2,1,0:T(8,128)(2,1)} %bitcast.107, bf16[6,1,9,8,128]{4,3,2,1,0:T(8,128)(2,1)} %bitcast.109, ...), custom_call_target="tpu_custom_call" | custom-call | tf_op jit(solution)/shard_map/step/pallas_call | solution.py:579
  307.8 13.2 %finish.1 = (bf16[9216,8,128]{2,1,0:T(8,128)(2,1)}, bf16[6,4,9,8,128]{4,3,2,1,0:T(8,128)(2,1)}, bf16[6,1,9,8,128]{4,3,2,1,0:T(8,128)(2,1)}, bf16[6,1,9,8,128]{4,...) custom-call(bf16[14400,8,128]{2,1,0:T(8,128)(2,1)S(1)} %get-tuple-el, ...), custom_call_target="tpu_custom_call" | custom-call | tf_op jit(solution)/shard_map/finish/pallas_call | solution.py:595
  321.0 0.7 slice.9
  321.7 0.8 slice.8
  322.5 0.6 reshape.138
  323.2 0.6 reshape.139

commit v3 on v2

--- a/solution.py
+++ b/solution.py
@@ -21,6 +21,7 @@
 CUT = (14, 13)
 NC = 9
 T = 33
+EARLY = 5
 STEP = 11
 MINI = 9
 EMB = 9216
@@ -30,19 +31,19 @@
 HALF = 2367
 HEAD = 21
 PUB = 900
-NA = 3
-PC = 100
+NA = 6
+PC = 50
 EXT = HEAD + SHARE
 OFF_Q, OFF_K, OFF_V, OFF_O = 369, 585, 639, 693
 OFF_G, OFF_U, OFF_D, OFF_N = 909, 2367, 3825, 5283
 DIM = (2, 4, 8)
 SHIFT = 88
-GRANT = 26300000
+GRANT = 26400000
 RAW_END = 12 * WIN
-OWN_AT = RAW_END
-RAW_M = OWN_AT + 12 * T
+RAW_M = RAW_END
 OWN_M = RAW_M + 9 * MINI
 STAGE_AT = OWN_M + 3 * MINI
+OWN_AT = STAGE_AT
 
 
 def start_of(s):
@@ -219,10 +220,18 @@
         pos = pos + count * size - over
 
 
-def step_kernel(emb, q, k, v, out, gate, up, down, norm, mom, var, mas, hyper,
+def norm_rows(fn):
+    for l in range(6):
+        for ct in range(9):
+            fn(0, l, ct * LANES, pl.ds(36 * l + ct, 4, 9))
+        for ct in range(2):
+            fn(1, l, ct * LANES, pl.ds(216 + 4 * l + ct, 2, 2))
+
+
+def step_kernel(emb, q, k, v, out, gate, up, down, norms, qk, mom, var, mas, hyper,
                 full, m_buf, v_buf, p_buf, lay,
-                acc, buf, recv3, tmp, part, acc_m, recv2_m, recv3_m,
-                lay_sem, state_sem, head_sems, own_sem, raw_send, raw_recv, s2_send, s2_recv, s3_send, s3_recv, n_send, n_recv,
+                norms_v, qk_v, acc, buf, recv3, tmp, part, acc_m, recv2_m, recv3_m,
+                norm_sem, lay_sem, state_sem, head_sems, own_sem, raw_send, raw_recv, s2_send, s2_recv, s3_send, s3_recv, n_send, n_recv,
                 m_raw_send, m_raw_recv, m_own, m_send, m_recv, a_send, a_recv, pair_recv):
     me = lax.axis_index("dp")
     core = me % 2
@@ -233,6 +242,12 @@
     loads = [pltpu.make_async_copy(src, dst.at[pl.ds(HEAD * ROWS, SHARE * ROWS)], state_sem.at[n]) for n, (src, dst) in enumerate(state)]
     for copy in loads:
         copy.start()
+    small = [pltpu.make_async_copy(src, dst, norm_sem.at[n]) for n, (src, dst) in enumerate(((norms, norms_v), (qk, qk_v)))]
+    for copy in small:
+        copy.start()
+    barrier = pltpu.get_barrier_semaphore()
+    loop(1, DEVICES, lambda n: pl.semaphore_signal(barrier, inc=1, device_id=(lax.rem(me + n, DEVICES),), device_id_type=MESH))
+    pl.semaphore_wait(barrier, DEVICES - 1)
     heads = [put(src.at[pl.ds((SHARE - HEAD) * ROWS, HEAD * ROWS)], dst.at[pl.ds(0, HEAD * ROWS)], head_sems.at[0, n], head_sems.at[1, n],
                  lax.rem(me + 1, DEVICES)) for n, (src, dst) in enumerate(state)]
 
@@ -268,9 +283,17 @@
 
             loop(0, 4, share_step)
 
-    loop(0, 3, lambda ch: scatter(ch, 1, 0))
+    rows2 = tmp.reshape(2 * LANES, LANES)
+
+    def norm_row(which, l, lane, at):
+        rows2[at, :] = (norms_v, qk_v)[which][l, :, lane:lane + LANES].astype(F32)
+
+    loop(0, EARLY, lambda ch: scatter(ch, 1, 0))
+    for copy in small:
+        copy.wait()
+    norm_rows(norm_row)
     for lo, whole, split in ((0, ((emb.at[pl.ds(TAIL, OFF_Q)], 0), (out, OFF_O)), ((q, OFF_Q, 4), (k, OFF_K, 1), (v, OFF_V, 1), (gate, OFF_G, 27))),
-                             (HALF, ((down, OFF_D), (norm, OFF_N)), ((up, OFF_U, 27),))):
+                             (HALF, ((down, OFF_D),), ((up, OFF_U, 27),))):
         n = HALF if lo == 0 else LAY - HALF
         stage = full.at[pl.ds(STAGE_AT, n)]
         for src, off in whole:
@@ -281,11 +304,15 @@
                 pltpu.make_async_copy(src.at[i // 9, :, lax.rem(i, 9)], full.at[pl.ds(STAGE_AT + off - lo + i * size, size)], lay_sem.at[0]).start()
 
         loop(0, 54, load)
-        copies_wait(stage, lay_sem.at[0])
+        if lo == 0:
+            copies_wait(stage, lay_sem.at[0])
+        else:
+            copies_wait(full.at[pl.ds(STAGE_AT, n - 30)], lay_sem.at[0])
+            full[pl.ds(STAGE_AT + n - 30, 30)] = rows2[pl.ds(0, 30 * ROWS), :].reshape((30,) + TILE).astype(BF16)
         save = pltpu.make_async_copy(stage, lay.at[pl.ds(lo, n)], lay_sem.at[1])
         save.start()
         save.wait()
-    loop(0, NC, lambda ch: scatter(ch, jnp.where(ch < 3, 0, 1), 1))
+    loop(0, NC, lambda ch: scatter(ch, jnp.where(ch < EARLY, 0, 1), 1))
 
     cut = jnp.where(core == 0, *CUT)
 
@@ -478,7 +505,7 @@
     mine = full.at[pl.ds(me * PUB, PUB)]
 
     def publish(c):
-        loop(jnp.where(c == 0, 0, 9 + 50 * c), jnp.minimum(59 + 50 * c, EXT // 6), update)
+        loop(jnp.where(c == 0, 0, 9 + PC // 2 * c), jnp.minimum(9 + PC // 2 * (c + 1), EXT // 6), update)
         walk_units(me, False, c * 3 * PC, (c + 1) * 3 * PC, TO_TILES, lambda fn, o: fn(mine, p_buf, tmp, o, base + o))
         for hop in range(3):
             for kc in range(3):
@@ -522,7 +549,7 @@
             copies_wait(acc_m.at[kc], m_send.at[kc])
 
 
-def finish_kernel(gathered, m, v, p, emb, q, k, v_out, out, gate, up, down, norm, mom_out, var_out, mas_out, sem, state_sem):
+def finish_kernel(gathered, m, v, p, emb, q, k, v_out, out, gate, up, down, norms, qk, mom_out, var_out, mas_out, norms_v, qk_v, rows2, sem, state_sem):
     starts = [9 * (SHARE * s // 9) - {13: 18, 14: 9}.get(s, 0) for s in range(16)] + [TAIL + LAY]
     state = [pltpu.make_async_copy(src.at[pl.ds(HEAD * ROWS, SHARE * ROWS)], dst, state_sem.at[n])
              for n, (src, dst) in enumerate(((m, mom_out), (v, var_out), (p, mas_out)))]
@@ -530,7 +557,7 @@
         copy.start()
     for dst, first, n, size in ((emb, 0, EMB, 1), (q, TAIL + OFF_Q, 54, 4), (k, TAIL + OFF_K, 54, 1), (v_out, TAIL + OFF_V, 54, 1),
                                 (out, TAIL + OFF_O, 216, 1), (gate, TAIL + OFF_G, 54, 27), (up, TAIL + OFF_U, 54, 27),
-                                (down, TAIL + OFF_D, 1458, 1), (norm, TAIL + OFF_N, 30, 1)):
+                                (down, TAIL + OFF_D, 1458, 1)):
         for s in range(16):
             lo, hi = max(starts[s], first), min(starts[s + 1], first + n * size)
             if lo >= hi:
@@ -547,8 +574,17 @@
                 return carry
 
             lax.fori_loop(0, (hi - lo) // size, step, 0)
-    copies_wait(gathered.at[pl.ds(0, TAIL + LAY)], sem)
-    for copy in state:
+    rows2[...] = gathered[pl.ds(15 * PUB + OFF_N - 4428, 30)].astype(F32).reshape(30 * ROWS, LANES)
+
+    def norm_row(which, l, lane, at):
+        (norms_v, qk_v)[which][l, :, lane:lane + LANES] = rows2[at, :].astype(BF16)
+
+    norm_rows(norm_row)
+    small = [pltpu.make_async_copy(src, dst, state_sem.at[3 + n]) for n, (src, dst) in enumerate(((norms_v, norms), (qk_v, qk)))]
+    for copy in small:
+        copy.start()
+    copies_wait(gathered.at[pl.ds(0, TAIL + OFF_N)], sem)
+    for copy in state + small:
         copy.wait()
 
 
@@ -572,32 +608,32 @@
         emb, q, k, v, out, gate, up, down, norms, qk = [a[0] for a in arrays[:GRAD_COUNT]]
         *state, hyper = arrays[GRAD_COUNT:]
         q_t, k_t, v_t, gate_t, up_t = [tiled(jnp.swapaxes(x, 1, 2)) for x in (q, k, v, gate, up)]
-        norm = jnp.concatenate([norms.reshape(-1), qk.reshape(-1)]).reshape((-1,) + TILE)
+        small = [pltpu.VMEM(x.shape, BF16) for x in (norms, qk)]
         rows = [x.reshape(SHARE * ROWS, LANES) for x in state]
-        args = [flat_tiles(emb), q_t, k_t, v_t, flat_tiles(out), gate_t, up_t, flat_tiles(down), norm] + rows
+        args = [flat_tiles(emb), q_t, k_t, v_t, flat_tiles(out), gate_t, up_t, flat_tiles(down), norms, qk] + rows
 
         *kept, _ = pl.pallas_call(
             step_kernel,
             out_shape=(pltpu.VMEM((DEVICES * PUB,) + TILE, BF16),) + (pltpu.VMEM((EXT * ROWS, LANES), F32),) * 3
             + (jax.ShapeDtypeStruct((LAYP,) + TILE, BF16),),
-            in_specs=[ANY] * 12 + [pl.BlockSpec(memory_space=pltpu.SMEM)],
+            in_specs=[ANY] * 13 + [pl.BlockSpec(memory_space=pltpu.SMEM)],
             out_specs=(VM,) * 4 + (ANY,),
-            scratch_shapes=[
+            scratch_shapes=small + [
                 pltpu.VMEM((3, NC, 4 * T) + TILE, F32), pltpu.VMEM((2 * WIDE,) + TILE, F32), pltpu.VMEM((WIN,) + TILE, F32),
                 pltpu.VMEM((2, LANES, LANES), F32), pltpu.VMEM((DEVICES,) + TILE, F32)]
             + [pltpu.VMEM((3, MINI) + TILE, F32)] * 3
-            + [DMA((2,)), DMA((3,)), DMA((2, 3)), DMA((3,)), DMA, DMA((3, NC)), DMA, DMA((3, NC)), DMA, DMA((3, NC)), DMA, DMA,
+            + [DMA((2,)), DMA((2,)), DMA((3,)), DMA((2, 3)), DMA((3,)), DMA, DMA((3, NC)), DMA, DMA((3, NC)), DMA, DMA((3, NC)), DMA, DMA,
                DMA((3, 2)), DMA((3,)), DMA, DMA((3,)), DMA((2, 3)), DMA, DMA((NA, 3, 7)), DMA],
-            compiler_params=pltpu.CompilerParams(has_side_effects=True, vmem_limit_bytes=GRANT),
+            compiler_params=pltpu.CompilerParams(collective_id=0, has_side_effects=True, vmem_limit_bytes=GRANT),
             name="step",
         )(*args, hyper)
 
-        emb2, q2, k2, v2, out2, gate2, up2, down2, norm2, *state2 = pl.pallas_call(
+        emb2, q2, k2, v2, out2, gate2, up2, down2, norms2, qk2, *state2 = pl.pallas_call(
             finish_kernel,
             out_shape=tuple(jax.ShapeDtypeStruct(x.shape, x.dtype) for x in args),
             in_specs=[VM] * 4,
-            out_specs=(ANY,) * 12,
-            scratch_shapes=[DMA, DMA((3,))],
+            out_specs=(ANY,) * 13,
+            scratch_shapes=small + [pltpu.VMEM((30 * ROWS, LANES), F32), DMA, DMA((5,))],
             compiler_params=pltpu.CompilerParams(vmem_limit_bytes=GRANT),
             name="finish",
         )(*[pltpu.with_memory_space_constraint(x, pltpu.VMEM) for x in kept])
@@ -609,10 +645,8 @@
         def columns(x, like):
             return jnp.swapaxes(matrices(x, jnp.swapaxes(like, 1, 2)), 1, 2)
 
-        flat_norm = norm2.reshape(-1)
-        cut = norms.size
         params = (matrices(emb2, emb), columns(q2, q), columns(k2, k), columns(v2, v), matrices(out2, out), columns(gate2, gate), columns(up2, up),
-                  matrices(down2, down), flat_norm[:cut].reshape(norms.shape), flat_norm[cut:].reshape(qk.shape))
+                  matrices(down2, down), norms2, qk2)
         return params + tuple(x.reshape(-1) for x in state2)
 
     in_specs = tuple([P("dp")] * GRAD_COUNT + [P("dp"), P("dp"), P("dp"), P()])

time: 324 us -> 312 us (0.963)
  Pallas kernels: 318 us -> 311 us
  local copies, waits for them, and re-layouts: 4.3 us -> 0 us
    pallas_call x1, Pallas kernels: 305 us -> 298 us  [local_update(): pl.pallas_call(step_kernel, out_shape=(pltpu.VMEM((DEVICES * PUB,) + TILE...]
where the time goes in v3:
time: 312 us
  Pallas kernels  311 us (100%)
    pallas_call x1, Pallas kernels, local_update(): pl.pallas_call(step_kernel, out_shape=(pltpu.VMEM((DEVICES * PUB,) + TILE...  298 us
    pallas_call x1, Pallas kernels, local_update(): pl.pallas_call(finish_kernel, out_shape=tuple((jax.ShapeDtypeStruct(x.sha...  13.2 us

profile of v3, /device:TPU:0, one launch (start us, length us, event | category | flops | bytes accessed | tf_op | source)
XLA Modules:
  0.0 311.9 jit_solution(15217096840364263772)
XLA Ops:
  0.7 298.0 %step.1 = (bf16[14400,8,128]{2,1,0:T(8,128)(2,1)S(1)}, f32[7248,128]{1,0:T(8,128)S(1)}, f32[7248,128]{1,0:T(8,128)S(1)}, f32[7248,128]{1,0:T(8,128)S(1)}, bf16[5322,8,128]{2,1,0:T(8,128)(2,1)}) custom-call(bf16[9216,8,128]{2,1,0:T(8,128)(2,1)} %bitcast.98, bf16[6,4,9,8,128]{4,3,2,1,0:T(8,128)(2,1)} %bitcast.105, bf16[6,1,9,8,128]{4,3,2,1,0:T(8,128)(2,1)} %bitcast.107, ...), custom_call_target="tpu_custom_call" | custom-call | tf_op jit(solution)/shard_map/step/pallas_call | solution.py:615
  298.6 13.2 %finish.1 = (bf16[9216,8,128]{2,1,0:T(8,128)(2,1)}, bf16[6,4,9,8,128]{4,3,2,1,0:T(8,128)(2,1)}, bf16[6,1,9,8,128]{4,3,2,1,0:T(8,128)(2,1)}, bf16[6,1,9,8,128]{4,...) custom-call(bf16[14400,8,128]{2,1,0:T(8,128)(2,1)S(1)} %get-tuple-el, ...), custom_call_target="tpu_custom_call" | custom-call | tf_op jit(solution)/shard_map/finish/pallas_call | solution.py:631

commit v4 on v3

--- a/solution.py
+++ b/solution.py
@@ -238,18 +238,14 @@
     pair = me + 1 - 2 * core
     flat = buf.reshape(2 * WIDE * ROWS, LANES)
 
-    state = ((mom, m_buf), (var, v_buf), (mas, p_buf))
-    loads = [pltpu.make_async_copy(src, dst.at[pl.ds(HEAD * ROWS, SHARE * ROWS)], state_sem.at[n]) for n, (src, dst) in enumerate(state)]
-    for copy in loads:
-        copy.start()
     small = [pltpu.make_async_copy(src, dst, norm_sem.at[n]) for n, (src, dst) in enumerate(((norms, norms_v), (qk, qk_v)))]
     for copy in small:
         copy.start()
     barrier = pltpu.get_barrier_semaphore()
-    loop(1, DEVICES, lambda n: pl.semaphore_signal(barrier, inc=1, device_id=(lax.rem(me + n, DEVICES),), device_id_type=MESH))
-    pl.semaphore_wait(barrier, DEVICES - 1)
-    heads = [put(src.at[pl.ds((SHARE - HEAD) * ROWS, HEAD * ROWS)], dst.at[pl.ds(0, HEAD * ROWS)], head_sems.at[0, n], head_sems.at[1, n],
-                 lax.rem(me + 1, DEVICES)) for n, (src, dst) in enumerate(state)]
+    peers = [pair] + [flip(me, dim) + to for dim in range(3) for to in (0, 1 - 2 * core)]
+    for peer in peers:
+        pl.semaphore_signal(barrier, inc=1, device_id=(peer,), device_id_type=MESH)
+    pl.semaphore_wait(barrier, len(peers))
 
     def raw_at(kc, ch, src, j):
         return full.at[pl.ds(((kc * NC + ch) * 12 + src * 4 + j) * T, T)]
@@ -313,6 +309,10 @@
         save.start()
         save.wait()
     loop(0, NC, lambda ch: scatter(ch, jnp.where(ch < EARLY, 0, 1), 1))
+    state = ((mom, m_buf), (var, v_buf), (mas, p_buf))
+    loads = [pltpu.make_async_copy(src, dst.at[pl.ds(HEAD * ROWS, SHARE * ROWS)], state_sem.at[n]) for n, (src, dst) in enumerate(state)]
+    for copy in loads:
+        copy.start()
 
     cut = jnp.where(core == 0, *CUT)
 
@@ -430,43 +430,55 @@
     def flat_rows(t):
         return pl.ds((WIDE + t) * ROWS, ROWS)
 
-    def squares(lo, hi, total):
-        def step(t, total):
-            for n in range(15):
-                x = flat[flat_rows(HEAD + t * 15 + n), :]
-                total = total + x * x
-            return total
-        return lax.fori_loop(lo, hi, step, total)
-
-    def ready(ch):
-        return jnp.maximum((ch * 3 * T - 48) // 15, 0)
+    published = jnp.where(me == 15, SHARE, start_of(me + 1) - start_of(me))
+
+    def squares(x, first):
+        ids = first + lax.broadcasted_iota(jnp.int32, x.shape, 0)
+        return jnp.sum(jnp.where(ids < published, x * x, 0.0), axis=0)
 
     def third_sum(ch, total):
+        to_flat((ch - 1) * 3 * T, ch * 3 * T)
         for kc in range(3):
             a, b, e = axes(kc)
             copies_wait(recv3.at[pl.ds((ch * 3 + kc) * T, T)], s3_recv.at[kc, ch])
 
-            def tile_step(t):
+            def tile_step(t, total):
                 i = pl.ds((ch * 3 + kc) * T + t * STEP, STEP)
-                buf[i] = (acc[kc, ch, pl.ds((2 * bit(me, b) + bit(me, e)) * T + t * STEP, STEP)] + recv3[i]) * 0.0625
-
-            loop(0, T // STEP, tile_step)
-        to_flat(ch * 3 * T, (ch + 1) * 3 * T)
-        return squares(ready(ch), ready(ch + 1), total)
+                x = (acc[kc, ch, pl.ds((2 * bit(me, b) + bit(me, e)) * T + t * STEP, STEP)] + recv3[i]) * 0.0625
+                buf[i] = x
+                return total + squares(x, (ch * 3 + kc) * T + t * STEP)
+
+            total = lax.fori_loop(0, T // STEP, tile_step, total)
+        return total
 
     total = lax.fori_loop(0, NC, third_sum, jnp.zeros(TILE, F32))
+    part[me] = jnp.sum(total, axis=0, keepdims=True)
 
     @pl.when(me == cut)
     def _():
+        extra = jnp.zeros(TILE, F32)
         for kc in range(3):
             copies_wait(recv3_m.at[kc], m_recv.at[1, kc])
-            buf[pl.ds(extra_at(kc), MINI)] = (acc_m[kc] + recv3_m[kc]) * 0.0625
-
-    to_flat(NC * 3 * T, 2 * WIDE)
-    part[me] = squares(ready(NC), SHARE // 15, total)
+            x = (acc_m[kc] + recv3_m[kc]) * 0.0625
+            buf[pl.ds(extra_at(kc), MINI)] = x
+            extra = extra + squares(x, extra_at(kc))
+        part[me] = part[me] + jnp.sum(extra, axis=0, keepdims=True)
+
     loop(1, DEVICES, lambda n: put(part.at[me], part.at[me], n_send, n_recv, lax.rem(me + n, DEVICES)))
 
-    for copy in loads + heads:
+    def heads(d, fn):
+        for many in (True, False):
+            n = HEAD if many else 6
+
+            @pl.when((d != 15) & (((d == 12) | (d == 13)) == many))
+            def _():
+                for m, (src, dst) in enumerate(state):
+                    fn(m, src.at[pl.ds((SHARE - n) * ROWS, n * ROWS)], dst.at[pl.ds((HEAD - n) * ROWS, n * ROWS)])
+
+    heads(me, lambda m, src, dst: put(src, dst, head_sems.at[0, m], head_sems.at[1, m], lax.rem(me + 1, DEVICES)))
+    to_flat((NC - 1) * 3 * T, 2 * WIDE)
+
+    for copy in loads:
         copy.wait()
 
     def fill(x):
@@ -481,8 +493,10 @@
     fix2 = 1.0 / (1.0 - power7(b2))
     others = pl.ds(0, DEVICES - 1)
     copies_wait(part.at[others], n_recv)
-    norm_sum = fill(jnp.sum(jnp.sum(part[...], axis=0)))
+    norm_sum = fill(jnp.sum(part[...]))
     clip = jnp.minimum(1.0, limit / (jnp.sqrt(norm_sum) + CLIP_EPS))
+
+    heads(lax.rem(me + 15, DEVICES), lambda m, src, dst: copies_wait(dst, head_sems.at[1, m]))
 
     def update(t):
         for n in range(6):
@@ -540,6 +554,7 @@
     copies_wait(buf.at[pl.ds(0, 2 * WIN)], s2_send)
     copies_wait(recv3, s3_send)
     copies_wait(part.at[others], n_send)
+    heads(me, lambda m, src, dst: copies_wait(dst, head_sems.at[0, m]))
     extra_sends(lambda kc, to, s, far: copies_wait(lay.at[pl.ds(0, MINI)], m_raw_send.at[kc, to]))
     for kc in range(3):
         a, b, e = axes(kc)
@@ -620,7 +635,7 @@
             out_specs=(VM,) * 4 + (ANY,),
             scratch_shapes=small + [
                 pltpu.VMEM((3, NC, 4 * T) + TILE, F32), pltpu.VMEM((2 * WIDE,) + TILE, F32), pltpu.VMEM((WIN,) + TILE, F32),
-                pltpu.VMEM((2, LANES, LANES), F32), pltpu.VMEM((DEVICES,) + TILE, F32)]
+                pltpu.VMEM((2, LANES, LANES), F32), pltpu.VMEM((DEVICES, 1, LANES), F32)]
             + [pltpu.VMEM((3, MINI) + TILE, F32)] * 3
             + [DMA((2,)), DMA((2,)), DMA((3,)), DMA((2, 3)), DMA((3,)), DMA, DMA((3, NC)), DMA, DMA((3, NC)), DMA, DMA((3, NC)), DMA, DMA,
                DMA((3, 2)), DMA((3,)), DMA, DMA((3,)), DMA((2, 3)), DMA, DMA((NA, 3, 7)), DMA],

time: 312 us -> 309 us (level)
    pallas_call x1, Pallas kernels: 298 us -> 295 us  [local_update(): pl.pallas_call(step_kernel, out_shape=(pltpu.VMEM((DEVICES * PUB,) + TILE...]
where the time goes in v4:
time: 309 us; the launch traced here: 308 us
  Pallas kernels  308 us (100%)
    pallas_call x1, Pallas kernels, local_update(): pl.pallas_call(step_kernel, out_shape=(pltpu.VMEM((DEVICES * PUB,) + TILE...  295 us
    pallas_call x1, Pallas kernels, local_update(): pl.pallas_call(finish_kernel, out_shape=tuple((jax.ShapeDtypeStruct(x.sha...  13.2 us

profile of v4, /device:TPU:0, one launch (start us, length us, event | category | flops | bytes accessed | tf_op | source)
XLA Modules:
  0.0 308.5 jit_solution(13666660534441726115)
XLA Ops:
  0.7 294.6 %step.1 = (bf16[14400,8,128]{2,1,0:T(8,128)(2,1)S(1)}, f32[7248,128]{1,0:T(8,128)S(1)}, f32[7248,128]{1,0:T(8,128)S(1)}, f32[7248,128]{1,0:T(8,128)S(1)}, bf16[5322,8,128]{2,1,0:T(8,128)(2,1)}) custom-call(bf16[9216,8,128]{2,1,0:T(8,128)(2,1)} %bitcast.98, bf16[6,4,9,8,128]{4,3,2,1,0:T(8,128)(2,1)} %bitcast.105, bf16[6,1,9,8,128]{4,3,2,1,0:T(8,128)(2,1)} %bitcast.107, ...), custom_call_target="tpu_custom_call" | custom-call | tf_op jit(solution)/shard_map/step/pallas_call | solution.py:630
  295.2 13.2 %finish.1 = (bf16[9216,8,128]{2,1,0:T(8,128)(2,1)}, bf16[6,4,9,8,128]{4,3,2,1,0:T(8,128)(2,1)}, bf16[6,1,9,8,128]{4,3,2,1,0:T(8,128)(2,1)}, bf16[6,1,9,8,128]{4,...) custom-call(bf16[14400,8,128]{2,1,0:T(8,128)(2,1)S(1)} %get-tuple-el, ...), custom_call_target="tpu_custom_call" | custom-call | tf_op jit(solution)/shard_map/finish/pallas_call | solution.py:646

commit v5 on v4

--- a/solution.py
+++ b/solution.py
@@ -31,8 +31,8 @@
 HALF = 2367
 HEAD = 21
 PUB = 900
-NA = 6
-PC = 50
+NA = 10
+PC = 30
 EXT = HEAD + SHARE
 OFF_Q, OFF_K, OFF_V, OFF_O = 369, 585, 639, 693
 OFF_G, OFF_U, OFF_D, OFF_N = 909, 2367, 3825, 5283
@@ -44,6 +44,7 @@
 OWN_M = RAW_M + 9 * MINI
 STAGE_AT = OWN_M + 3 * MINI
 OWN_AT = STAGE_AT
+BLOCK, COLS, BLOCKS, SCALES = 27, 216, 54, 30
 
 
 def start_of(s):
@@ -86,12 +87,12 @@
 
 def gate_segments():
     rows = []
-    for kap in range(27):
+    for kap in range(BLOCK):
         pieces, f = [], LANES * kap
         while f < LANES * (kap + 1):
-            i, c = f // 216, f % 216
+            i, c = f // COLS, f % COLS
             pieces.append((f - LANES * kap, i, c // LANES))
-            f = min(LANES * (kap + 1), 216 * i + (LANES if c < LANES else 216))
+            f = min(LANES * (kap + 1), COLS * i + (LANES if c < LANES else COLS))
         rows.append(pieces)
     return rows
 
@@ -140,7 +141,7 @@
         val = None
         for lo, i, half in pieces:
             val = rolled[i, half] if val is None else jnp.where(ids >= lo, rolled[i, half], val)
-        flat[pl.ds(f * ROWS + kap, ROWS, 27), :] = val
+        flat[pl.ds(f * ROWS + kap, ROWS, BLOCK), :] = val
 
 
 def q_to_flat(win, flat, tmp, o, f):
@@ -169,7 +170,7 @@
 
 def gate_to_tiles(stage, flat, tmp, o, f):
     ids = lanes()
-    rows = [flat[pl.ds(f * ROWS + kap, ROWS, 27), :] for kap in range(27)]
+    rows = [flat[pl.ds(f * ROWS + kap, ROWS, BLOCK), :] for kap in range(BLOCK)]
     for (i, half), pieces in gate_inverse().items():
         val = rows[pieces[0][2]]
         for lo, hi, kap in pieces[1:]:
@@ -212,7 +213,7 @@
     second = pick({10: 22 if wide else 21, 14: 67})
     pos = 0
     for count, size, fn, over in ((first, 9, rows9, 0), (pick({10: 14}), 16, q, pick({10: 8})), (pick({10: 7}), 16, kv, pick({10: 4})),
-                                  (n_gate, 27, gate, 0), (second, 9, rows9, 0), (pick({15: 30}), 1, one, 0)):
+                                  (n_gate, BLOCK, gate, 0), (second, 9, rows9, 0), (pick({15: SCALES}), 1, one, 0)):
         def done(x):
             return jnp.minimum(jnp.maximum(x - pos + (0 if wide else size - 1), 0) // size, count)
 
@@ -225,20 +226,21 @@
         for ct in range(9):
             fn(0, l, ct * LANES, pl.ds(36 * l + ct, 4, 9))
         for ct in range(2):
-            fn(1, l, ct * LANES, pl.ds(216 + 4 * l + ct, 2, 2))
-
-
-def step_kernel(emb, q, k, v, out, gate, up, down, norms, qk, mom, var, mas, hyper,
+            fn(1, l, ct * LANES, pl.ds(COLS + 4 * l + ct, 2, 2))
+
+
+def step_kernel(emb, q, k, v, out, gate, up, down, norms, qk, mom, var, mas, hyper_in,
                 full, m_buf, v_buf, p_buf, lay,
-                norms_v, qk_v, acc, buf, recv3, tmp, part, acc_m, recv2_m, recv3_m,
-                norm_sem, lay_sem, state_sem, head_sems, own_sem, raw_send, raw_recv, s2_send, s2_recv, s3_send, s3_recv, n_send, n_recv,
-                m_raw_send, m_raw_recv, m_own, m_send, m_recv, a_send, a_recv, pair_recv):
+                hyper, norms_v, qk_v, acc, buf, recv3, tmp, part, acc_m, recv2_m, recv3_m,
+                norm_sem, lay_sem, state_sem, head_sems, own_sem, recv_sems, raw_send, s2_send, s3_send, n_send, n_recv,
+                m_raw_send, m_raw_recv, m_own, m_send, m_recv, a_send, pair_recv, hyper_sem):
     me = lax.axis_index("dp")
     core = me % 2
     pair = me + 1 - 2 * core
     flat = buf.reshape(2 * WIDE * ROWS, LANES)
 
     small = [pltpu.make_async_copy(src, dst, norm_sem.at[n]) for n, (src, dst) in enumerate(((norms, norms_v), (qk, qk_v)))]
+    small.append(pltpu.make_async_copy(hyper_in, hyper, hyper_sem))
     for copy in small:
         copy.start()
     barrier = pltpu.get_barrier_semaphore()
@@ -247,6 +249,12 @@
         pl.semaphore_signal(barrier, inc=1, device_id=(peer,), device_id_type=MESH)
     pl.semaphore_wait(barrier, len(peers))
 
+    def hop_sem(hop, ch):
+        return recv_sems.at[hop * NC + ch]
+
+    def piece_sem(c, piece):
+        return recv_sems.at[c * 7 + piece]
+
     def raw_at(kc, ch, src, j):
         return full.at[pl.ds(((kc * NC + ch) * 12 + src * 4 + j) * T, T)]
 
@@ -265,7 +273,7 @@
         def one(s, kc, src, j, target):
             @pl.when(jnp.where(s < 10, with_emb, with_lay) == 1)
             def _():
-                share_tiles(s, (ch * 3 + kc) * T, T, lambda ref: put(ref, raw_at(kc, ch, src, j), raw_send, raw_recv.at[kc, ch], target))
+                share_tiles(s, (ch * 3 + kc) * T, T, lambda ref: put(ref, raw_at(kc, ch, src, j), raw_send, hop_sem(0, ch), target))
 
         for kc in range(3):
             a, b, e = axes(kc)
@@ -288,8 +296,8 @@
     for copy in small:
         copy.wait()
     norm_rows(norm_row)
-    for lo, whole, split in ((0, ((emb.at[pl.ds(TAIL, OFF_Q)], 0), (out, OFF_O)), ((q, OFF_Q, 4), (k, OFF_K, 1), (v, OFF_V, 1), (gate, OFF_G, 27))),
-                             (HALF, ((down, OFF_D),), ((up, OFF_U, 27),))):
+    for lo, whole, split in ((0, ((emb.at[pl.ds(TAIL, OFF_Q)], 0), (out, OFF_O)), ((q, OFF_Q, 4), (k, OFF_K, 1), (v, OFF_V, 1), (gate, OFF_G, BLOCK))),
+                             (HALF, ((down, OFF_D),), ((up, OFF_U, BLOCK),))):
         n = HALF if lo == 0 else LAY - HALF
         stage = full.at[pl.ds(STAGE_AT, n)]
         for src, off in whole:
@@ -299,12 +307,12 @@
             for src, off, size in split:
                 pltpu.make_async_copy(src.at[i // 9, :, lax.rem(i, 9)], full.at[pl.ds(STAGE_AT + off - lo + i * size, size)], lay_sem.at[0]).start()
 
-        loop(0, 54, load)
+        loop(0, BLOCKS, load)
         if lo == 0:
             copies_wait(stage, lay_sem.at[0])
         else:
-            copies_wait(full.at[pl.ds(STAGE_AT, n - 30)], lay_sem.at[0])
-            full[pl.ds(STAGE_AT + n - 30, 30)] = rows2[pl.ds(0, 30 * ROWS), :].reshape((30,) + TILE).astype(BF16)
+            copies_wait(full.at[pl.ds(STAGE_AT, n - SCALES)], lay_sem.at[0])
+            full[pl.ds(STAGE_AT + n - SCALES, SCALES)] = rows2[pl.ds(0, SCALES * ROWS), :].reshape((SCALES,) + TILE).astype(BF16)
         save = pltpu.make_async_copy(stage, lay.at[pl.ds(lo, n)], lay_sem.at[1])
         save.start()
         save.wait()
@@ -346,9 +354,9 @@
         fetch(0, kc)
 
     def first_sum(ch):
+        copies_wait(full.at[pl.ds(0, 36 * T)], hop_sem(0, ch))
         for kc in range(3):
             a, b, e = axes(kc)
-            copies_wait(full.at[pl.ds((kc * NC + ch) * 12 * T, 12 * T)], raw_recv.at[kc, ch])
             copies_wait(full.at[pl.ds(OWN_AT + kc * 4 * T, 4 * T)], own_sem.at[kc])
 
             def sum_step(n):
@@ -364,7 +372,7 @@
 
             loop(0, 4, sum_step)
             put(acc.at[kc, ch, pl.ds(2 * (1 - bit(me, b)) * T, 2 * T)], buf.at[pl.ds((kc * NC + ch) * 2 * T, 2 * T)],
-                s2_send, s2_recv.at[kc, ch], flip(me, b))
+                s2_send, hop_sem(1, ch), flip(me, b))
 
             @pl.when(ch + 1 < NC)
             def _():
@@ -396,10 +404,10 @@
                 put(acc_m.at[kc], recv2_m.at[kc], m_send.at[kc], m_recv.at[0, kc], flip(me, b))
 
     def second_sum(ch):
+        copies_wait(buf.at[pl.ds(0, 6 * T)], hop_sem(1, ch))
         for kc in range(3):
             a, b, e = axes(kc)
             slot = (kc * NC + ch) * 2 * T
-            copies_wait(buf.at[pl.ds(slot, 2 * T)], s2_recv.at[kc, ch])
             for je in ((1 - bit(me, e)), bit(me, e)):
                 def tile_step(t):
                     at = pl.ds((2 * bit(me, b) + je) * T + t * STEP, STEP)
@@ -407,7 +415,7 @@
 
                 loop(0, T // STEP, tile_step)
             put(acc.at[kc, ch, pl.ds((2 * bit(me, b) + 1 - bit(me, e)) * T, T)], recv3.at[pl.ds((ch * 3 + kc) * T, T)],
-                s3_send, s3_recv.at[kc, ch], flip(me, e))
+                s3_send, hop_sem(2, ch), flip(me, e))
 
     loop(0, NC, second_sum)
     for kc in range(3):
@@ -438,9 +446,9 @@
 
     def third_sum(ch, total):
         to_flat((ch - 1) * 3 * T, ch * 3 * T)
+        copies_wait(recv3.at[pl.ds(ch * 3 * T, 3 * T)], hop_sem(2, ch))
         for kc in range(3):
             a, b, e = axes(kc)
-            copies_wait(recv3.at[pl.ds((ch * 3 + kc) * T, T)], s3_recv.at[kc, ch])
 
             def tile_step(t, total):
                 i = pl.ds((ch * 3 + kc) * T + t * STEP, STEP)
@@ -518,31 +526,34 @@
 
     mine = full.at[pl.ds(me * PUB, PUB)]
 
+    def made(c):
+        return (c * 3 * PC + BLOCKS) // 6
+
     def publish(c):
-        loop(jnp.where(c == 0, 0, 9 + PC // 2 * c), jnp.minimum(9 + PC // 2 * (c + 1), EXT // 6), update)
+        loop(jnp.where(c == 0, 0, made(c)), jnp.minimum(made(c + 1), EXT // 6), update)
         walk_units(me, False, c * 3 * PC, (c + 1) * 3 * PC, TO_TILES, lambda fn, o: fn(mine, p_buf, tmp, o, base + o))
         for hop in range(3):
             for kc in range(3):
                 dim = axes(kc)[hop]
-                send(me, c, kc, flip(me, dim), a_recv.at[c, kc, (0, 1, 3)[hop]])
+                send(me, c, kc, flip(me, dim), piece_sem(c, (0, 1, 3)[hop]))
         for kc in range(3):
             send(me, c, kc, pair, pair_recv)
 
     loop(0, NA, publish)
 
     def pass_on(level, c):
-        for kc in range(3):
-            a, b, e = axes(kc)
-            for n in ((1,), (2, 3), (4, 5, 6, 7))[level]:
+        for n in ((1,), (2, 3), (4, 5, 6, 7))[level]:
+            copies_wait(full.at[pl.ds(0, 3 * PC)], piece_sem(c, n - 1))
+            for kc in range(3):
+                a, b, e = axes(kc)
                 owner = me
                 for pos, dim in enumerate((a, b, e)):
                     if (n >> pos) & 1:
                         owner = flip(owner, dim)
-                copies_wait(full.at[pl.ds(owner * PUB + (c * 3 + kc) * PC, PC)], a_recv.at[c, kc, n - 1])
                 if level == 0:
-                    send(owner, c, kc, flip(me, b), a_recv.at[c, kc, 2])
+                    send(owner, c, kc, flip(me, b), piece_sem(c, 2))
                 if level < 2:
-                    send(owner, c, kc, flip(me, e), a_recv.at[c, kc, n + 3])
+                    send(owner, c, kc, flip(me, e), piece_sem(c, n + 3))
                 send(owner, c, kc, pair, pair_recv)
 
     for level in range(3):
@@ -570,8 +581,8 @@
              for n, (src, dst) in enumerate(((m, mom_out), (v, var_out), (p, mas_out)))]
     for copy in state:
         copy.start()
-    for dst, first, n, size in ((emb, 0, EMB, 1), (q, TAIL + OFF_Q, 54, 4), (k, TAIL + OFF_K, 54, 1), (v_out, TAIL + OFF_V, 54, 1),
-                                (out, TAIL + OFF_O, 216, 1), (gate, TAIL + OFF_G, 54, 27), (up, TAIL + OFF_U, 54, 27),
+    for dst, first, n, size in ((emb, 0, EMB, 1), (q, TAIL + OFF_Q, BLOCKS, 4), (k, TAIL + OFF_K, BLOCKS, 1), (v_out, TAIL + OFF_V, BLOCKS, 1),
+                                (out, TAIL + OFF_O, COLS, 1), (gate, TAIL + OFF_G, BLOCKS, BLOCK), (up, TAIL + OFF_U, BLOCKS, BLOCK),
                                 (down, TAIL + OFF_D, 1458, 1)):
         for s in range(16):
             lo, hi = max(starts[s], first), min(starts[s + 1], first + n * size)
@@ -589,7 +600,7 @@
                 return carry
 
             lax.fori_loop(0, (hi - lo) // size, step, 0)
-    rows2[...] = gathered[pl.ds(15 * PUB + OFF_N - 4428, 30)].astype(F32).reshape(30 * ROWS, LANES)
+    rows2[...] = gathered[pl.ds(15 * PUB + OFF_N - 4428, SCALES)].astype(F32).reshape(SCALES * ROWS, LANES)
 
     def norm_row(which, l, lane, at):
         (norms_v, qk_v)[which][l, :, lane:lane + LANES] = rows2[at, :].astype(BF16)
@@ -631,14 +642,14 @@
             step_kernel,
             out_shape=(pltpu.VMEM((DEVICES * PUB,) + TILE, BF16),) + (pltpu.VMEM((EXT * ROWS, LANES), F32),) * 3
             + (jax.ShapeDtypeStruct((LAYP,) + TILE, BF16),),
-            in_specs=[ANY] * 13 + [pl.BlockSpec(memory_space=pltpu.SMEM)],
+            in_specs=[ANY] * 14,
             out_specs=(VM,) * 4 + (ANY,),
-            scratch_shapes=small + [
+            scratch_shapes=[pltpu.SMEM(hyper.shape, F32)] + small + [
                 pltpu.VMEM((3, NC, 4 * T) + TILE, F32), pltpu.VMEM((2 * WIDE,) + TILE, F32), pltpu.VMEM((WIN,) + TILE, F32),
                 pltpu.VMEM((2, LANES, LANES), F32), pltpu.VMEM((DEVICES, 1, LANES), F32)]
             + [pltpu.VMEM((3, MINI) + TILE, F32)] * 3
-            + [DMA((2,)), DMA((2,)), DMA((3,)), DMA((2, 3)), DMA((3,)), DMA, DMA((3, NC)), DMA, DMA((3, NC)), DMA, DMA((3, NC)), DMA, DMA,
-               DMA((3, 2)), DMA((3,)), DMA, DMA((3,)), DMA((2, 3)), DMA, DMA((NA, 3, 7)), DMA],
+            + [DMA((2,)), DMA((2,)), DMA((3,)), DMA((2, 3)), DMA((3,)), DMA((max(3 * NC, 7 * NA),)), DMA, DMA, DMA, DMA, DMA,
+               DMA((3, 2)), DMA((3,)), DMA, DMA((3,)), DMA((2, 3)), DMA, DMA, DMA],
             compiler_params=pltpu.CompilerParams(collective_id=0, has_side_effects=True, vmem_limit_bytes=GRANT),
             name="step",
         )(*args, hyper)
@@ -648,7 +659,7 @@
             out_shape=tuple(jax.ShapeDtypeStruct(x.shape, x.dtype) for x in args),
             in_specs=[VM] * 4,
             out_specs=(ANY,) * 13,
-            scratch_shapes=small + [pltpu.VMEM((30 * ROWS, LANES), F32), DMA, DMA((5,))],
+            scratch_shapes=small + [pltpu.VMEM((SCALES * ROWS, LANES), F32), DMA, DMA((5,))],
             compiler_params=pltpu.CompilerParams(vmem_limit_bytes=GRANT),
             name="finish",
         )(*[pltpu.with_memory_space_constraint(x, pltpu.VMEM) for x in kept])

time: 309 us -> 306 us (level)
    pallas_call x1, Pallas kernels: 295 us -> 291 us  [local_update(): pl.pallas_call(step_kernel, out_shape=(pltpu.VMEM((DEVICES * PUB,) + TILE...]
where the time goes in v5:
time: 306 us; the launch traced here: 305 us
  Pallas kernels  305 us (100%)
    pallas_call x1, Pallas kernels, local_update(): pl.pallas_call(step_kernel, out_shape=(pltpu.VMEM((DEVICES * PUB,) + TILE...  291 us
    pallas_call x1, Pallas kernels, local_update(): pl.pallas_call(finish_kernel, out_shape=tuple((jax.ShapeDtypeStruct(x.sha...  13.2 us

profile of v5, /device:TPU:0, one launch (start us, length us, event | category | flops | bytes accessed | tf_op | source)
XLA Modules:
  0.0 305.2 jit_solution(18011402033352226469)
XLA Ops:
  0.7 291.3 %step.1 = (bf16[14400,8,128]{2,1,0:T(8,128)(2,1)S(1)}, f32[7248,128]{1,0:T(8,128)S(1)}, f32[7248,128]{1,0:T(8,128)S(1)}, f32[7248,128]{1,0:T(8,128)S(1)}, bf16[5322,8,128]{2,1,0:T(8,128)(2,1)}) custom-call(bf16[9216,8,128]{2,1,0:T(8,128)(2,1)} %bitcast.98, bf16[6,4,9,8,128]{4,3,2,1,0:T(8,128)(2,1)} %bitcast.105, bf16[6,1,9,8,128]{4,3,2,1,0:T(8,128)(2,1)} %bitcast.107, ...), custom_call_target="tpu_custom_call" | custom-call | tf_op jit(solution)/shard_map/step/pallas_call | solution.py:641
  291.9 13.2 %finish.1 = (bf16[9216,8,128]{2,1,0:T(8,128)(2,1)}, bf16[6,4,9,8,128]{4,3,2,1,0:T(8,128)(2,1)}, bf16[6,1,9,8,128]{4,3,2,1,0:T(8,128)(2,1)}, bf16[6,1,9,8,128]{4,...) custom-call(bf16[14400,8,128]{2,1,0:T(8,128)(2,1)S(1)} %get-tuple-el, ...), custom_call_target="tpu_custom_call" | custom-call | tf_op jit(solution)/shard_map/finish/pallas_call | solution.py:657

commit v6 on v5

--- a/solution.py
+++ b/solution.py
@@ -29,11 +29,13 @@
 LAY = 5313
 LAYP = LAY + MINI
 HALF = 2367
-HEAD = 21
-PUB = 900
-NA = 10
-PC = 30
-EXT = HEAD + SHARE
+HEAD = 6
+LAST = 12
+FLAT = WIDE + 15
+PUB = 891
+NA = 9
+PC = 33
+EXT = HEAD + SHARE + LAST
 OFF_Q, OFF_K, OFF_V, OFF_O = 369, 585, 639, 693
 OFF_G, OFF_U, OFF_D, OFF_N = 909, 2367, 3825, 5283
 DIM = (2, 4, 8)
@@ -49,6 +51,10 @@
 
 def start_of(s):
     return 9 * ((SHARE * s) // 9) - jnp.where(s == 13, 18, 0) - jnp.where(s == 14, 9, 0)
+
+
+def skip_of(s):
+    return jnp.where((s == 13) | (s == 14), BLOCK, 0)
 
 
 def axes(colour):
@@ -209,7 +215,7 @@
     rows9, gate, q, kv, one = fns
     ends = (SHARE * (me + 1) + (8 if wide else 0)) // 9 - (SHARE * me) // 9
     first = jnp.where(me < 10, ends, pick({10: 41, 11: 3, 15: 95}))
-    n_gate = pick({11: 32, 12: 33 if wide else 32, 13: 34 if wide else 33, 14: 11})
+    n_gate = pick({11: 32, 12: 33, 13: 34, 14: 11})
     second = pick({10: 22 if wide else 21, 14: 67})
     pos = 0
     for count, size, fn, over in ((first, 9, rows9, 0), (pick({10: 14}), 16, q, pick({10: 8})), (pick({10: 7}), 16, kv, pick({10: 4})),
@@ -433,16 +439,17 @@
     base = HEAD - (SHARE * me - start_of(me))
 
     def to_flat(lo, hi):
-        walk_units(me, True, lo, hi, TO_FLAT, lambda fn, o: fn(buf, flat, tmp, o, WIDE + base + o))
+        walk_units(me, True, lo, hi, TO_FLAT, lambda fn, o: fn(buf, flat, tmp, o, FLAT + base + o))
 
     def flat_rows(t):
-        return pl.ds((WIDE + t) * ROWS, ROWS)
-
-    published = jnp.where(me == 15, SHARE, start_of(me + 1) - start_of(me))
+        return pl.ds((FLAT + t) * ROWS, ROWS)
+
+    skip = skip_of(me)
+    last = jnp.where(me == 15, SHARE, start_of(me + 1) + skip_of(me + 1) - start_of(me))
 
     def squares(x, first):
         ids = first + lax.broadcasted_iota(jnp.int32, x.shape, 0)
-        return jnp.sum(jnp.where(ids < published, x * x, 0.0), axis=0)
+        return jnp.sum(jnp.where((ids >= skip) & (ids < last), x * x, 0.0), axis=0)
 
     def third_sum(ch, total):
         to_flat((ch - 1) * 3 * T, ch * 3 * T)
@@ -474,16 +481,24 @@
 
     loop(1, DEVICES, lambda n: put(part.at[me], part.at[me], n_send, n_recv, lax.rem(me + n, DEVICES)))
 
-    def heads(d, fn):
-        for many in (True, False):
-            n = HEAD if many else 6
-
-            @pl.when((d != 15) & (((d == 12) | (d == 13)) == many))
+    def ends(cases, fn):
+        for who, *case in cases:
+            @pl.when(who)
             def _():
-                for m, (src, dst) in enumerate(state):
-                    fn(m, src.at[pl.ds((SHARE - n) * ROWS, n * ROWS)], dst.at[pl.ds((HEAD - n) * ROWS, n * ROWS)])
-
-    heads(me, lambda m, src, dst: put(src, dst, head_sems.at[0, m], head_sems.at[1, m], lax.rem(me + 1, DEVICES)))
+                fn(*case)
+
+    sent = ((me < 12, 0, HEAD), (me == 13, 1, HEAD), (me == 14, 1, LAST))
+    got = (((me > 0) & (me < 13), 0, HEAD), (me == 12, 1, HEAD), (me == 13, 1, LAST))
+
+    def end_put(kind, n):
+        at, to, target = ((SHARE - n, 0, me + 1), (0, HEAD + SHARE, me - 1))[kind]
+        for src, dst in state:
+            put(src.at[pl.ds(at * ROWS, n * ROWS)], dst.at[pl.ds(to * ROWS, n * ROWS)], head_sems.at[0, kind], head_sems.at[1, kind], target)
+
+    def end_wait(side, kind, n):
+        copies_wait(m_buf.at[pl.ds(0, 3 * n * ROWS)], head_sems.at[side, kind])
+
+    ends(sent, end_put)
     to_flat((NC - 1) * 3 * T, 2 * WIDE)
 
     for copy in loads:
@@ -504,11 +519,11 @@
     norm_sum = fill(jnp.sum(part[...]))
     clip = jnp.minimum(1.0, limit / (jnp.sqrt(norm_sum) + CLIP_EPS))
 
-    heads(lax.rem(me + 15, DEVICES), lambda m, src, dst: copies_wait(dst, head_sems.at[1, m]))
+    ends(got, functools.partial(end_wait, 1))
 
     def update(t):
-        for n in range(6):
-            tile = t * 6 + n
+        for n in range(7):
+            tile = t * 7 + n
             i = pl.ds(tile * ROWS, ROWS)
             h = flat[flat_rows(tile), :] * clip
             pt = p_buf[i, :]
@@ -527,11 +542,11 @@
     mine = full.at[pl.ds(me * PUB, PUB)]
 
     def made(c):
-        return (c * 3 * PC + BLOCKS) // 6
+        return (c * 3 * PC + 51) // 7
 
     def publish(c):
-        loop(jnp.where(c == 0, 0, made(c)), jnp.minimum(made(c + 1), EXT // 6), update)
-        walk_units(me, False, c * 3 * PC, (c + 1) * 3 * PC, TO_TILES, lambda fn, o: fn(mine, p_buf, tmp, o, base + o))
+        loop(jnp.where(c == 0, 0, made(c)), jnp.minimum(made(c + 1), EXT // 7), update)
+        walk_units(me, False, skip + c * 3 * PC, skip + (c + 1) * 3 * PC, TO_TILES, lambda fn, o: fn(mine, p_buf, tmp, o - skip, base + o))
         for hop in range(3):
             for kc in range(3):
                 dim = axes(kc)[hop]
@@ -565,7 +580,7 @@
     copies_wait(buf.at[pl.ds(0, 2 * WIN)], s2_send)
     copies_wait(recv3, s3_send)
     copies_wait(part.at[others], n_send)
-    heads(me, lambda m, src, dst: copies_wait(dst, head_sems.at[0, m]))
+    ends(sent, functools.partial(end_wait, 0))
     extra_sends(lambda kc, to, s, far: copies_wait(lay.at[pl.ds(0, MINI)], m_raw_send.at[kc, to]))
     for kc in range(3):
         a, b, e = axes(kc)
@@ -576,7 +591,7 @@
 
 
 def finish_kernel(gathered, m, v, p, emb, q, k, v_out, out, gate, up, down, norms, qk, mom_out, var_out, mas_out, norms_v, qk_v, rows2, sem, state_sem):
-    starts = [9 * (SHARE * s // 9) - {13: 18, 14: 9}.get(s, 0) for s in range(16)] + [TAIL + LAY]
+    starts = [9 * (SHARE * s // 9) + {13: 9, 14: 18}.get(s, 0) for s in range(16)] + [TAIL + LAY]
     state = [pltpu.make_async_copy(src.at[pl.ds(HEAD * ROWS, SHARE * ROWS)], dst, state_sem.at[n])
              for n, (src, dst) in enumerate(((m, mom_out), (v, var_out), (p, mas_out)))]
     for copy in state:
@@ -648,7 +663,7 @@
                 pltpu.VMEM((3, NC, 4 * T) + TILE, F32), pltpu.VMEM((2 * WIDE,) + TILE, F32), pltpu.VMEM((WIN,) + TILE, F32),
                 pltpu.VMEM((2, LANES, LANES), F32), pltpu.VMEM((DEVICES, 1, LANES), F32)]
             + [pltpu.VMEM((3, MINI) + TILE, F32)] * 3
-            + [DMA((2,)), DMA((2,)), DMA((3,)), DMA((2, 3)), DMA((3,)), DMA((max(3 * NC, 7 * NA),)), DMA, DMA, DMA, DMA, DMA,
+            + [DMA((2,)), DMA((2,)), DMA((3,)), DMA((2, 2)), DMA((3,)), DMA((max(3 * NC, 7 * NA),)), DMA, DMA, DMA, DMA, DMA,
                DMA((3, 2)), DMA((3,)), DMA, DMA((3,)), DMA((2, 3)), DMA, DMA, DMA],
             compiler_params=pltpu.CompilerParams(collective_id=0, has_side_effects=True, vmem_limit_bytes=GRANT),
             name="step",

time: 306 us -> 304 us (level)
  no operation moved by 1% of the time
where the time goes in v6:
time: 304 us
  Pallas kernels  303 us (100%)
    pallas_call x1, Pallas kernels, local_update(): pl.pallas_call(step_kernel, out_shape=(pltpu.VMEM((DEVICES * PUB,) + TILE...  290 us
    pallas_call x1, Pallas kernels, local_update(): pl.pallas_call(finish_kernel, out_shape=tuple((jax.ShapeDtypeStruct(x.sha...  13.2 us

profile of v6, /device:TPU:0, one launch (start us, length us, event | category | flops | bytes accessed | tf_op | source)
XLA Modules:
  0.0 304.1 jit_solution(14844050807542618503)
XLA Ops:
  0.7 290.2 %step.1 = (bf16[14256,8,128]{2,1,0:T(8,128)(2,1)S(1)}, f32[7224,128]{1,0:T(8,128)S(1)}, f32[7224,128]{1,0:T(8,128)S(1)}, f32[7224,128]{1,0:T(8,128)S(1)}, bf16[5322,8,128]{2,1,0:T(8,128)(2,1)}) custom-call(bf16[9216,8,128]{2,1,0:T(8,128)(2,1)} %bitcast.98, bf16[6,4,9,8,128]{4,3,2,1,0:T(8,128)(2,1)} %bitcast.105, bf16[6,1,9,8,128]{4,3,2,1,0:T(8,128)(2,1)} %bitcast.107, ...), custom_call_target="tpu_custom_call" | custom-call | tf_op jit(solution)/shard_map/step/pallas_call | solution.py:656
  290.9 13.2 %finish.1 = (bf16[9216,8,128]{2,1,0:T(8,128)(2,1)}, bf16[6,4,9,8,128]{4,3,2,1,0:T(8,128)(2,1)}, bf16[6,1,9,8,128]{4,3,2,1,0:T(8,128)(2,1)}, bf16[6,1,9,8,128]{4,...) custom-call(bf16[14256,8,128]{2,1,0:T(8,128)(2,1)S(1)} %get-tuple-el, ...), custom_call_target="tpu_custom_call" | custom-call | tf_op jit(solution)/shard_map/finish/pallas_call | solution.py:672

commit v7 on v6

--- a/solution.py
+++ b/solution.py
@@ -335,7 +335,7 @@
 
     def extra_sends(fn):
         for kc in range(3):
-            for to, s in enumerate(CUT):
+            for to, s in list(enumerate(CUT))[min(kc, 1):]:
                 far = bit(me, kc) != bit(s, kc)
 
                 @pl.when(far | (core != to))
@@ -387,7 +387,7 @@
     loop(0, NC, first_sum)
 
     def near(*dims):
-        same = bit(me, dims[0]) == bit(cut, dims[0])
+        same = (bit(me, dims[0]) == bit(cut, dims[0])) & (core >= min(dims[0], 1))
         for dim in dims[1:]:
             same = same & (bit(me, dim) == bit(cut, dim))
         return same
@@ -469,15 +469,13 @@
     total = lax.fori_loop(0, NC, third_sum, jnp.zeros(TILE, F32))
     part[me] = jnp.sum(total, axis=0, keepdims=True)
 
-    @pl.when(me == cut)
-    def _():
-        extra = jnp.zeros(TILE, F32)
-        for kc in range(3):
+    for kc in range(3):
+        @pl.when((me == cut) & (core >= min(kc, 1)))
+        def _():
             copies_wait(recv3_m.at[kc], m_recv.at[1, kc])
             x = (acc_m[kc] + recv3_m[kc]) * 0.0625
             buf[pl.ds(extra_at(kc), MINI)] = x
-            extra = extra + squares(x, extra_at(kc))
-        part[me] = part[me] + jnp.sum(extra, axis=0, keepdims=True)
+            part[me] = part[me] + jnp.sum(squares(x, extra_at(kc)), axis=0, keepdims=True)
 
     loop(1, DEVICES, lambda n: put(part.at[me], part.at[me], n_send, n_recv, lax.rem(me + n, DEVICES)))
 

time: 304 us -> 304 us (level)
  no operation moved by 1% of the time
where the time goes in v7:
time: 304 us; the launch traced here: 303 us
  Pallas kernels  303 us (100%)
    pallas_call x1, Pallas kernels, local_update(): pl.pallas_call(step_kernel, out_shape=(pltpu.VMEM((DEVICES * PUB,) + TILE...  289 us
    pallas_call x1, Pallas kernels, local_update(): pl.pallas_call(finish_kernel, out_shape=tuple((jax.ShapeDtypeStruct(x.sha...  13.2 us

profile of v7, /device:TPU:0, one launch (start us, length us, event | category | flops | bytes accessed | tf_op | source)
XLA Modules:
  0.0 303.2 jit_solution(13024124234631741386)
XLA Ops:
  0.7 289.4 %step.1 = (bf16[14256,8,128]{2,1,0:T(8,128)(2,1)S(1)}, f32[7224,128]{1,0:T(8,128)S(1)}, f32[7224,128]{1,0:T(8,128)S(1)}, f32[7224,128]{1,0:T(8,128)S(1)}, bf16[5322,8,128]{2,1,0:T(8,128)(2,1)}) custom-call(bf16[9216,8,128]{2,1,0:T(8,128)(2,1)} %bitcast.98, bf16[6,4,9,8,128]{4,3,2,1,0:T(8,128)(2,1)} %bitcast.105, bf16[6,1,9,8,128]{4,3,2,1,0:T(8,128)(2,1)} %bitcast.107, ...), custom_call_target="tpu_custom_call" | custom-call | tf_op jit(solution)/shard_map/step/pallas_call | solution.py:654
  290.0 13.2 %finish.1 = (bf16[9216,8,128]{2,1,0:T(8,128)(2,1)}, bf16[6,4,9,8,128]{4,3,2,1,0:T(8,128)(2,1)}, bf16[6,1,9,8,128]{4,3,2,1,0:T(8,128)(2,1)}, bf16[6,1,9,8,128]{4,...) custom-call(bf16[14256,8,128]{2,1,0:T(8,128)(2,1)S(1)} %get-tuple-el, ...), custom_call_target="tpu_custom_call" | custom-call | tf_op jit(solution)/shard_map/finish/pallas_call | solution.py:670
